TPU v7x, 32 devices: a whole 2x2x4 slice. The times are simulated.
32 devices in a mesh: ctx: 16 (over z, x, core), head: 2 (over y).
Axes of the slice: x: 2, y: 2, z: 4, core: 2. Of those that a mesh axis runs over, the one named last changes fastest.
Arguments:
- queries: bfloat16 [4096, 1024], P('ctx', 'head'), may hold values from -6 to 6
- keys: bfloat16 [4096, 1024], P('ctx', 'head'), may hold values from -6 to 6
- values: bfloat16 [4096, 1024], P('ctx', 'head'), may hold values from -6 to 6
- out_grad: bfloat16 [4096, 1024], P('ctx', 'head'), may hold values from -48 to 48
- outputs: bfloat16 [4096, 1024], P('ctx', 'head'), may hold values from -1.5 to 1.5
- log_norms: float32 [4096, 8], P('ctx', 'head'), may hold values from 4 to 7
- selected: int32 [32, 8, 3], P('ctx', 'head'), may hold values from -1 to 29, as said below
Outputs:
- grad_queries: bfloat16 [4096, 1024], P(('ctx', 'head'))
- grad_keys: bfloat16 [4096, 1024], P('ctx', 'head')
- grad_values: bfloat16 [4096, 1024], P('ctx', 'head')
Inputs may be any that keep to these rules, and one draw needn't show every extreme that they name: `selected`: -1 marks no block; every other entry is a block held by a lower index of ctx than the query block's own, and the entries other than -1 of one query block and head differ. Among all entries of one index of ctx and one group of 4 heads, at most 2 name blocks held by any one other index of ctx; blocks may repeat across query blocks and heads.
All inputs are finite; a program needn't handle non-finite values.
Results may differ from a plain program's by a relative error of at most 0.0057.
Values may be sent and summed in bfloat16 or wider, within the bound.
A program may use at most 64 MiB of HBM per device.

v0:
```python
import jax
import jax.numpy as jnp
from jax import lax
from jax.sharding import PartitionSpec as P

PER_PEER = 2


def to_pairs(matrix, blocks, heads):
    row_count, full_width = matrix.shape
    block_len = row_count // blocks
    head_dim = full_width // heads
    shaped = matrix.reshape(blocks, block_len, heads, head_dim)
    return jnp.transpose(shaped, (0, 2, 1, 3)).reshape(blocks * heads, block_len, head_dim)


def stat_pairs(matrix, blocks):
    row_count, heads = matrix.shape
    shaped = matrix.reshape(blocks, row_count // blocks, heads)
    return jnp.transpose(shaped, (0, 2, 1)).reshape(blocks * heads, row_count // blocks)


def from_pairs(pairs, blocks, heads):
    block_len, head_dim = (pairs.shape[1], pairs.shape[2])
    shaped = pairs.reshape(blocks, heads, block_len, head_dim)
    return jnp.transpose(shaped, (0, 2, 1, 3)).reshape(blocks * block_len, heads * head_dim)


def pair_grads(query_rows, key_rows, value_rows, grad_rows, norms, deltas, factor, causal):
    block_scores = (
        jnp.einsum("nsd,ntd->nst", query_rows, key_rows, preferred_element_type=jnp.float32)
        * factor
    )
    weights = jnp.exp(block_scores - norms[:, :, None])
    if causal:
        position = jnp.arange(block_scores.shape[1])
        lower = position[:, None] >= position[None, :]
        weights = jnp.where(lower[None], weights, 0.0)
    dweights = jnp.einsum("nsd,ntd->nst", grad_rows, value_rows, preferred_element_type=jnp.float32)
    dscores = weights * (dweights - deltas[:, :, None])
    weights_b = weights.astype(jnp.bfloat16)
    dscores_b = dscores.astype(jnp.bfloat16)
    grad_v = jnp.einsum("nst,nsd->ntd", weights_b, grad_rows, preferred_element_type=jnp.float32)
    grad_k = (
        jnp.einsum("nst,nsd->ntd", dscores_b, query_rows, preferred_element_type=jnp.float32)
        * factor
    )
    grad_q = (
        jnp.einsum("nst,ntd->nsd", dscores_b, key_rows, preferred_element_type=jnp.float32) * factor
    )
    return (grad_q, grad_k, grad_v)


def live_order(live, group):
    order = jnp.argsort(1 - live.astype(jnp.int32), stable=True)
    turns = (jnp.sum(live.astype(jnp.int32)) + group - 1) // group
    return (order, turns)


def one_hot(targets, alive, pair_count):
    hits = (jnp.arange(pair_count, dtype=jnp.int32)[:, None] == targets[None, :]) & alive[None, :]
    return hits.astype(jnp.bfloat16)


def shards(queries, keys, values, out_grad, outputs, log_norms, selected):
    blocks, heads, top_count = selected.shape
    row_count, full_width = queries.shape
    head_dim = full_width // heads
    pair_count = blocks * heads
    factor = head_dim ** (-0.5)
    ctx_count = lax.axis_size("ctx")
    own_index = lax.axis_index("ctx")
    group = min(8, ctx_count)
    slot_total = ctx_count * PER_PEER
    query_pairs = to_pairs(queries, blocks, heads)
    key_pairs = to_pairs(keys, blocks, heads)
    value_pairs = to_pairs(values, blocks, heads)
    grad_pairs = to_pairs(out_grad, blocks, heads)
    delta_rows = jnp.sum(
        (out_grad.astype(jnp.float32) * outputs.astype(jnp.float32)).reshape(
            row_count, heads, head_dim
        ),
        axis=2,
    )
    norm_pairs = stat_pairs(log_norms, blocks)
    delta_pairs = stat_pairs(delta_rows, blocks)
    block_len = query_pairs.shape[1]
    grad_q, grad_k, grad_v = pair_grads(
        query_pairs, key_pairs, value_pairs, grad_pairs, norm_pairs, delta_pairs, factor, True
    )
    table = lax.all_gather(selected, "ctx", axis=0, tiled=True).reshape(
        ctx_count, pair_count * top_count
    )
    select_count = table.shape[1]
    select_ids = jnp.arange(select_count, dtype=jnp.int32)
    place_ids = jnp.arange(slot_total, dtype=jnp.int32)
    mine = selected.reshape(select_count)
    mine_owner = jnp.where(mine >= 0, mine // blocks, -1)
    same_owner = (mine_owner[:, None] == mine_owner[None, :]) & (mine_owner[None, :] >= 0)
    before = select_ids[None, :] < select_ids[:, None]
    mine_rank = jnp.sum((same_owner & before).astype(jnp.int32), axis=1)
    mine_place = jnp.where(mine_owner >= 0, mine_owner * PER_PEER + mine_rank, -1)
    place_match = mine_place[None, :] == place_ids[:, None]
    mine_live = jnp.any(place_match, axis=1)
    mine_query = jnp.sum(jnp.where(place_match, select_ids[None, :], 0), axis=1) // top_count
    theirs_match = (table >= 0) & (table // blocks == own_index)
    theirs_rank = jnp.cumsum(theirs_match.astype(jnp.int32), axis=1) - 1
    live_parts = []
    select_parts = []
    block_parts = []
    for slot_rank in range(PER_PEER):
        slot_hit = theirs_match & (theirs_rank == slot_rank)
        live_parts.append(jnp.any(slot_hit, axis=1))
        select_parts.append(jnp.sum(jnp.where(slot_hit, select_ids[None, :], 0), axis=1))
        block_parts.append(jnp.sum(jnp.where(slot_hit, table % blocks, 0), axis=1))
    theirs_live = jnp.stack(live_parts, axis=1).reshape(slot_total)
    theirs_select = jnp.stack(select_parts, axis=1).reshape(slot_total)
    theirs_block = jnp.stack(block_parts, axis=1).reshape(slot_total)
    theirs_key = theirs_block * heads + theirs_select // top_count % heads
    empty_pairs = jnp.zeros((pair_count, block_len, head_dim), jnp.float32)
    packed = jnp.concatenate([query_pairs, grad_pairs], axis=2)
    outgoing = jnp.where(mine_live[:, None, None], packed[mine_query], jnp.zeros((), jnp.bfloat16))
    stats = jnp.stack([norm_pairs[mine_query], delta_pairs[mine_query]], axis=1)
    stats = jnp.where(mine_live[:, None, None], stats, 0.0)
    arrived = lax.all_to_all(outgoing, "ctx", split_axis=0, concat_axis=0, tiled=True)
    arrived_stats = lax.all_to_all(stats, "ctx", split_axis=0, concat_axis=0, tiled=True)
    order, turns = live_order(theirs_live, group)

    def owner_turn(turn, carry):
        acc_k, acc_v, partial_value = carry
        picked = lax.dynamic_slice_in_dim(order, turn * group, group)
        alive = theirs_live[picked]
        target = theirs_key[picked]
        rows_in = arrived[picked]
        stats_in = arrived_stats[picked]
        part_q, part_k, part_v = pair_grads(
            rows_in[:, :, :head_dim],
            key_pairs[target],
            value_pairs[target],
            rows_in[:, :, head_dim:],
            stats_in[:, 0],
            stats_in[:, 1],
            factor,
            False,
        )
        hits = one_hot(target, alive, pair_count)
        acc_k = acc_k + jnp.einsum(
            "pg,gsd->psd", hits, part_k.astype(jnp.bfloat16), preferred_element_type=jnp.float32
        )
        acc_v = acc_v + jnp.einsum(
            "pg,gsd->psd", hits, part_v.astype(jnp.bfloat16), preferred_element_type=jnp.float32
        )
        rounded = jnp.where(
            alive[:, None, None], part_q.astype(jnp.bfloat16), jnp.zeros((), jnp.bfloat16)
        )
        partial_value = partial_value.at[picked].set(rounded)
        return (acc_k, acc_v, partial_value)

    empty_slots = jnp.zeros((slot_total, block_len, head_dim), jnp.bfloat16)
    acc_k, acc_v, partial_value = lax.fori_loop(
        0, turns, owner_turn, (empty_pairs, empty_pairs, empty_slots)
    )
    returned = lax.all_to_all(partial_value, "ctx", split_axis=0, concat_axis=0, tiled=True)
    grad_q = grad_q + jnp.einsum(
        "pc,csd->psd",
        one_hot(mine_query, mine_live, pair_count),
        returned,
        preferred_element_type=jnp.float32,
    )
    grad_k = grad_k + acc_k
    grad_v = grad_v + acc_v
    final_q = from_pairs(grad_q, blocks, heads).astype(jnp.bfloat16)
    final_k = from_pairs(grad_k, blocks, heads).astype(jnp.bfloat16)
    final_v = from_pairs(grad_v, blocks, heads).astype(jnp.bfloat16)
    spread_q = lax.all_to_all(final_q, "head", split_axis=0, concat_axis=1, tiled=True)
    return (spread_q, final_k, final_v)


def solution(mesh):
    placed = (
        P("ctx", "head"),
        P("ctx", "head"),
        P("ctx", "head"),
        P("ctx", "head"),
        P("ctx", "head"),
        P("ctx", "head"),
        P("ctx", "head", None),
    )
    return jax.shard_map(
        shards,
        mesh=mesh,
        in_specs=placed,
        out_specs=(P(("ctx", "head"), None), P("ctx", "head"), P("ctx", "head")),
        check_vma=False,
    )
```

profile of v0, /device:TPU:0, one launch (start us, length us, event | category | flops | bytes accessed | tf_op | source)
XLA Modules:
  0.0 167.6 jit_solution(3359445380577094043)
XLA Ops:
  0.7 0.8 copy.107
  2.0 1.1 convert_multiply_fusion
  5.7 7.4 %all-to-all-start.1 = ((f32[32,2,128]{2,1,0:T(2,128)}), f32[32,2,128]{2,1,0:T(2,128)S(1)}, u32[]{:S(2)}, u32[]{:S(2)}) async-start(f32[32,2,128]{2,1,0:T(2,128)} %copy.113), calls=%async_computation.1 | async-start | bytes 65536 | tf_op jit(solution)/shard_map/all_to_all | solution.py:126
  14.1 0.7 gather_fusion.6
  14.8 1.5 broadcast_select_fusion
  16.3 3.4 %all-to-all-done.1 = f32[32,2,128]{2,1,0:T(2,128)S(1)} async-done(((f32[32,2,128]{2,1,0:T(2,128)}), f32[32,2,128]{2,1,0:T(2,128)S(1)}, u32[]{:S(2)}, u32[]{:S(2)}) %all-to-all-start.1) | async-done | bytes 32800 | tf_op jit(solution)/shard_map/all_to_all | solution.py:126
  19.7 4.4 %all-to-all-start = ((bf16[32,128,256]{2,1,0:T(8,128)(2,1)}), bf16[32,128,256]{2,1,0:T(8,128)(2,1)}, u32[]{:S(2)}, u32[]{:S(2)}) async-start(bf16[32,128,256]{2,1,0:T(8,128)(2,1)} %broadcast_select_fusion), calls=%async_computation | async-start | bytes 4194304 | tf_op jit(solution)/shard_map/all_to_all | solution.py:125
  24.1 50.6 %all_gather.3 = s32[32,4,3]{2,1,0:T(4,128)S(1)} all-gather(s32[2,4,3]{2,1,0:T(4,128)S(1)} %copy.107), channel_id=1, replica_groups=mesh['ctx'=16,'head'=2] {'ctx'}, dimensions={0}, use_global_device_ids=true | all-gather | bytes 1632 | tf_op jit(solution)/shard_map/all_gather | solution.py:91
  75.3 2.4 %select_reduce_fusion.1 = (s32[32]{0:T(128)S(1)}, s32[32]{0:T(128)S(1)}, s32[32]{0:T(128)S(1)}, s32[32]{0:T(128)S(1)}, pred[32,4,3]{2,1,0:T(4,128)(4,1)S(1)}) fusion(s32[32,4,3]{2,1,0:T(4,128)S(1)} %all_gather.3, pred[32,4,3]{2,1,0:T(4,128)(4,1)S(1)} %eq.105, pred[32,4,3]{2,1,0:T(4,128)(4,1)S(1)} %eq.107, s32[2,4,3]{2,1,0:T(4,128)S(1)} %multiply_add_fusion, ...), kind=kLoop, calls=%fused_computation.77 | loop fusion | flops 12160 | bytes 3300 | tf_op jit(solution)/shard_map/reduce_sum | solution.py:115
  77.7 1.2 and_reduce_fusion.1
  79.3 0.6 convert_reduce_fusion.1
  82.6 1.6 sort.17
  84.3 1.2 broadcast_in_dim.148
  85.6 38.4 %while.14 = (s32[]{:T(128)}, f32[8,128,128]{2,0,1:T(8,128)S(1)}, f32[8,128,128]{2,0,1:T(8,128)S(1)}, bf16[32,128,128]{2,1,0:T(8,128)(2,1)}, s32[]{:T(128)}, /*in...) while((s32[]{:T(128)}, f32[8,128,128]{2,0,1:T(8,128)S(1)}, ...), condition=%wide.region_21.22_spmd, body=%wide.region_19.21_spmd.sunk | while | flops 173803824 | bytes 10535695 | solution.py:160
  87.0 2.2 %gather_fusion.3 = bf16[8,128,256]{2,1,0:T(8,128)(2,1)S(1)} fusion(bf16[32,128,256]{2,1,0:T(8,128)(2,1)} %get-tuple-element.291, s32[1024]{0:T(1024)S(1)} %pad_clamp_fusion.5), kind=kCustom, calls=%fused_computation.2.clone.1 | custom fusion | bytes 1048608 | tf_op jit(solution)/shard_map/while/body/gather | solution.py:134
  91.0 0.6 gather_fusion.5
  91.8 2.2 %scatter_fusion = bf16[32,128,128]{2,1,0:T(8,128)(2,1)} fusion(bf16[32,128,128]{2,1,0:T(8,128)(2,1)} %get-tuple-element.270, s32[8]{0:T(128)S(1)} %compare_select_fusion.11, bf16[8,128,128]{2,1,0:T(8,128)(2,1)S(1)} %fusion.107), kind=kCustom, calls=%fused_computation.9.clone.1 | custom fusion | bytes 786464 | tf_op jit(solution)/shard_map/while/body/scatter | solution.py:156
  96.6 2.2 %gather_fusion.3 = bf16[8,128,256]{2,1,0:T(8,128)(2,1)S(1)} fusion(bf16[32,128,256]{2,1,0:T(8,128)(2,1)} %get-tuple-element.291, s32[1024]{0:T(1024)S(1)} %pad_clamp_fusion.5), kind=kCustom, calls=%fused_computation.2.clone.1 | custom fusion | bytes 1048608 | tf_op jit(solution)/shard_map/while/body/gather | solution.py:134
  101.5 2.2 %scatter_fusion = bf16[32,128,128]{2,1,0:T(8,128)(2,1)} fusion(bf16[32,128,128]{2,1,0:T(8,128)(2,1)} %get-tuple-element.270, s32[8]{0:T(128)S(1)} %compare_select_fusion.11, bf16[8,128,128]{2,1,0:T(8,128)(2,1)S(1)} %fusion.107), kind=kCustom, calls=%fused_computation.9.clone.1 | custom fusion | bytes 786464 | tf_op jit(solution)/shard_map/while/body/scatter | solution.py:156
  106.2 2.2 %gather_fusion.3 = bf16[8,128,256]{2,1,0:T(8,128)(2,1)S(1)} fusion(bf16[32,128,256]{2,1,0:T(8,128)(2,1)} %get-tuple-element.291, s32[1024]{0:T(1024)S(1)} %pad_clamp_fusion.5), kind=kCustom, calls=%fused_computation.2.clone.1 | custom fusion | bytes 1048608 | tf_op jit(solution)/shard_map/while/body/gather | solution.py:134
  110.2 0.6 gather_fusion.5
  111.0 2.2 %scatter_fusion = bf16[32,128,128]{2,1,0:T(8,128)(2,1)} fusion(bf16[32,128,128]{2,1,0:T(8,128)(2,1)} %get-tuple-element.270, s32[8]{0:T(128)S(1)} %compare_select_fusion.11, bf16[8,128,128]{2,1,0:T(8,128)(2,1)S(1)} %fusion.107), kind=kCustom, calls=%fused_computation.9.clone.1 | custom fusion | bytes 786464 | tf_op jit(solution)/shard_map/while/body/scatter | solution.py:156
  115.7 2.2 %gather_fusion.3 = bf16[8,128,256]{2,1,0:T(8,128)(2,1)S(1)} fusion(bf16[32,128,256]{2,1,0:T(8,128)(2,1)} %get-tuple-element.291, s32[1024]{0:T(1024)S(1)} %pad_clamp_fusion.5), kind=kCustom, calls=%fused_computation.2.clone.1 | custom fusion | bytes 1048608 | tf_op jit(solution)/shard_map/while/body/gather | solution.py:134
  120.6 2.2 %scatter_fusion = bf16[32,128,128]{2,1,0:T(8,128)(2,1)} fusion(bf16[32,128,128]{2,1,0:T(8,128)(2,1)} %get-tuple-element.270, s32[8]{0:T(128)S(1)} %compare_select_fusion.11, bf16[8,128,128]{2,1,0:T(8,128)(2,1)S(1)} %fusion.107), kind=kCustom, calls=%fused_computation.9.clone.1 | custom fusion | bytes 786464 | tf_op jit(solution)/shard_map/while/body/scatter | solution.py:156
  124.0 8.4 %all-to-all-start.2 = ((bf16[32,128,128]{2,1,0:T(8,128)(2,1)}), bf16[32,128,128]{2,1,0:T(8,128)(2,1)S(1)}, u32[]{:S(2)}, u32[]{:S(2)}) async-start(bf16[32,128,128]{2,1,0:T(8,128)(2,1)} %get-tuple-element.70), calls=%async_computation.2 | async-start | bytes 2097152 | tf_op jit(solution)/shard_map/all_to_all | solution.py:163
  134.1 21.1 %all-to-all-done.2 = bf16[32,128,128]{2,1,0:T(8,128)(2,1)S(1)} async-done(((bf16[32,128,128]{2,1,0:T(8,128)(2,1)}), bf16[32,128,128]{2,1,0:T(8,128)(2,1)S(1)}, u32[]{:S(2)}, u32[]{:S(2)}) %all-to-all-start.2) | async-done | bytes 1048608 | tf_op jit(solution)/shard_map/all_to_all | solution.py:163
  155.3 0.7 fusion.33
  156.2 0.9 copy.118
  157.0 3.4 %all-to-all-start.3 = ((bf16[2,128,512]{1,2,0:T(8,128)(2,1)}), bf16[2,128,512]{1,2,0:T(8,128)(2,1)S(1)}, u32[]{:S(2)}, u32[]{:S(2)}) async-start(bf16[2,128,512]{1,2,0:T(8,128)(2,1)} %bitcast.42), calls=%async_computation.3 | async-start | bytes 524288 | tf_op jit(solution)/shard_map/all_to_all | solution.py:175
  160.5 0.9 copy_bitcast_fusion
  161.3 5.4 %all-to-all-done.3 = bf16[2,128,512]{1,2,0:T(8,128)(2,1)S(1)} async-done(((bf16[2,128,512]{1,2,0:T(8,128)(2,1)}), bf16[2,128,512]{1,2,0:T(8,128)(2,1)S(1)}, u32[]{:S(2)}, u32[]{:S(2)}) %all-to-all-start.3) | async-done | bytes 262176 | tf_op jit(solution)/shard_map/all_to_all | solution.py:175
  166.8 0.8 copy.125
  (153 shorter events, 27.9 us)
Async XLA Ops:
  0.6 12.4 %copy-start.5 = (bf16[256,512]{1,0:T(8,128)(2,1)S(1)}, bf16[256,512]{1,0:T(8,128)(2,1)}, u32[]{:S(2)}) copy-start(bf16[256,512]{1,0:T(8,128)(2,1)} %param.12) | copy-start | bytes 786436
  0.6 3.7 %copy-start = (f32[256,4]{0,1:T(4,128)S(1)}, f32[256,4]{0,1:T(4,128)}, u32[]{:S(2)}) copy-start(f32[256,4]{0,1:T(4,128)} %param.14) | copy-start | bytes 12292
  2.0 11.2 %copy-start.6 = (bf16[256,512]{1,0:T(8,128)(2,1)S(1)}, bf16[256,512]{1,0:T(8,128)(2,1)}, u32[]{:S(2)}) copy-start(bf16[256,512]{1,0:T(8,128)(2,1)} %param.9) | copy-start | bytes 786436
  5.7 14.0 %all-to-all-start.1 = ((f32[32,2,128]{2,1,0:T(2,128)}), f32[32,2,128]{2,1,0:T(2,128)S(1)}, u32[]{:S(2)}, u32[]{:S(2)}) async-start(f32[32,2,128]{2,1,0:T(2,128)} %copy.113), calls=%async_computation.1 | async-start | bytes 65536 | tf_op jit(solution)/shard_map/all_to_all | solution.py:126
  13.2 0.7 copy-start.1
  13.3 0.7 copy-start.3
  16.3 66.0 %copy-start.7 = (bf16[256,512]{1,0:T(8,128)(2,1)S(1)}, bf16[256,512]{1,0:T(8,128)(2,1)}, u32[]{:S(2)}) copy-start(bf16[256,512]{1,0:T(8,128)(2,1)} %param.10) | copy-start | bytes 786436
  16.3 66.2 %copy-start.8 = (bf16[256,512]{1,0:T(8,128)(2,1)S(1)}, bf16[256,512]{1,0:T(8,128)(2,1)}, u32[]{:S(2)}) copy-start(bf16[256,512]{1,0:T(8,128)(2,1)} %param.11) | copy-start | bytes 786436
  19.7 64.6 %all-to-all-start = ((bf16[32,128,256]{2,1,0:T(8,128)(2,1)}), bf16[32,128,256]{2,1,0:T(8,128)(2,1)}, u32[]{:S(2)}, u32[]{:S(2)}) async-start(bf16[32,128,256]{2,1,0:T(8,128)(2,1)} %broadcast_select_fusion), calls=%async_computation | async-start | bytes 4194304 | tf_op jit(solution)/shard_map/all_to_all | solution.py:125
  124.0 8.4 %copy-start.4 = (bf16[2,4,128,128]{3,2,1,0:T(8,128)(2,1)S(1)}, bf16[2,4,128,128]{3,2,1,0:T(8,128)(2,1)}, u32[]{:S(2)}) copy-start(bf16[2,4,128,128]{3,2,1,0:T(8,128)(2,1)} %copy-done.3) | copy-start | bytes 786436
  124.0 8.7 %copy-start.2 = (bf16[2,4,128,128]{3,2,1,0:T(8,128)(2,1)S(1)}, bf16[2,4,128,128]{3,2,1,0:T(8,128)(2,1)}, u32[]{:S(2)}) copy-start(bf16[2,4,128,128]{3,2,1,0:T(8,128)(2,1)} %copy-done.1) | copy-start | bytes 786436
  124.0 31.2 %all-to-all-start.2 = ((bf16[32,128,128]{2,1,0:T(8,128)(2,1)}), bf16[32,128,128]{2,1,0:T(8,128)(2,1)S(1)}, u32[]{:S(2)}, u32[]{:S(2)}) async-start(bf16[32,128,128]{2,1,0:T(8,128)(2,1)} %get-tuple-element.70), calls=%async_computation.2 | async-start | bytes 2097152 | tf_op jit(solution)/shard_map/all_to_all | solution.py:163
  157.0 9.7 %all-to-all-start.3 = ((bf16[2,128,512]{1,2,0:T(8,128)(2,1)}), bf16[2,128,512]{1,2,0:T(8,128)(2,1)S(1)}, u32[]{:S(2)}, u32[]{:S(2)}) async-start(bf16[2,128,512]{1,2,0:T(8,128)(2,1)} %bitcast.42), calls=%async_computation.3 | async-start | bytes 524288 | tf_op jit(solution)/shard_map/all_to_all | solution.py:175
where the time goes:
time: 169 us; the launch traced here: 168 us
  blocking collectives  50.6 us (30%)
  local copies, waits for them, and re-layouts  40.3 us (24%)
  waiting for transfers between devices  30 us (18%)
  starting transfers between devices  23.6 us (14%)
  other arithmetic  10.9 us (6%)
  matrix products  10 us (6%)
  between operations  1.77 us (1%)
    all_gather x1, blocking collectives, shards(): lax.all_gather(selected, 'ctx', axis=0, tiled=True)  50.6 us
    all_to_all x1, waiting for transfers between devices, shards(): lax.all_to_all(partial_value, 'ctx', split_axis=0, concat_axis=0, tiled=T...  21.1 us
    scatter x4, local copies, waits for them, and re-layouts, owner_turn(): partial_value = partial_value.at[picked].set(rounded)  8.78 us
    gather x4, local copies, waits for them, and re-layouts, owner_turn(): rows_in = arrived[picked]  8.68 us
    all_to_all x1, starting transfers between devices, shards(): lax.all_to_all(partial_value, 'ctx', split_axis=0, concat_axis=0, tiled=T...  8.35 us
    all_to_all x1, starting transfers between devices, shards(): lax.all_to_all(stats, 'ctx', split_axis=0, concat_axis=0, tiled=True)  7.39 us
    all_to_all x1, waiting for transfers between devices, shards(): lax.all_to_all(final_q, 'head', split_axis=0, concat_axis=1, tiled=True)  5.44 us
    all_to_all x1, starting transfers between devices, shards(): lax.all_to_all(outgoing, 'ctx', split_axis=0, concat_axis=0, tiled=True)  4.42 us
  transfers between devices with their start and end apart: 4, of which 3 were waited for; matrix products, arithmetic and copies ran while one was open for 8% of the time, Pallas kernels for 0%

commit v1 on v0

v1 whole, which is shorter than its diff:
```python
import functools

import jax
import jax.numpy as jnp
from jax import lax
from jax.experimental import pallas as pl
from jax.experimental.pallas import tpu as pltpu
from jax.sharding import PartitionSpec as P

GROUP = 4
JOBS_STEP = 4
MESH_ID = pl.DeviceIdType.MESH
NT = (((1,), (1,)), ((), ()))
NN = (((1,), (0,)), ((), ()))


def gather_kernel(levels, q_ref, g_ref, k_ref, v_ref, m_ref, a_buf, b_buf, m_buf, send_sem, recv_sem):
    me = lax.axis_index("ctx")
    head = lax.axis_index("head")
    level = me // GROUP
    col = me % GROUP
    colx = (col + 2) % GROUP
    colc = col + 1 - 2 * (col % 2)
    down_dev = me - GROUP
    up_dev = me + GROUP
    x_dev = level * GROUP + colx
    c_dev = level * GROUP + colc
    bufs = (a_buf, b_buf, m_buf)
    down_own = (q_ref, g_ref, m_ref)
    up_own = (k_ref, v_ref, m_ref)
    has_down = level > 0
    has_up = level < levels - 1

    barrier = pltpu.get_barrier_semaphore()

    def greet(dev):
        pl.semaphore_signal(barrier, inc=1, device_id=(dev, head), device_id_type=MESH_ID)

    greet(x_dev)
    greet(c_dev)

    @pl.when(has_down)
    def _():
        greet(down_dev)

    @pl.when(has_up)
    def _():
        greet(up_dev)

    pl.semaphore_wait(barrier, 2 + has_down.astype(jnp.int32) + has_up.astype(jnp.int32))

    def copy(way, part, slot, src, dev):
        return pltpu.make_async_remote_copy(
            src_ref=src,
            dst_ref=bufs[part].at[slot],
            send_sem=send_sem.at[way, part, slot],
            recv_sem=recv_sem.at[part, slot],
            device_id=(dev, head),
            device_id_type=MESH_ID,
        )

    def push(way, slot, dev, own=None):
        for part in (2, 0, 1):
            src = bufs[part].at[slot] if own is None else own[part]
            copy(way, part, slot, src, dev).start()

    def push_part(way, part, slot, dev):
        copy(way, part, slot, bufs[part].at[slot], dev).start()

    def arrive(part, slot):
        copy(0, part, slot, bufs[part].at[slot], c_dev).wait_recv()

    def sent(way, slot):
        for part in range(3):
            copy(way, part, slot, bufs[part].at[slot], c_dev).wait_send()

    @pl.when(has_down)
    def _():
        push(0, me, down_dev, down_own)

    @pl.when(has_up)
    def _():
        push(3, me, up_dev, up_own)

    @pl.when(col >= 2)
    def _():
        push(1, me, x_dev, down_own)

    @pl.when(col < 2)
    def _():
        push(1, me, x_dev, up_own)

    @pl.when(col % 2 == 1)
    def _():
        push(2, me, c_dev, down_own)

    @pl.when(col % 2 == 0)
    def _():
        push(2, me, c_dev, up_own)

    def cross(other):
        slot = other * GROUP + colx
        for part in (2, 0, 1):
            arrive(part, slot)
            push_part(2, part, slot, c_dev)

    def step(dist, carry):
        high = level + dist
        low = level - dist

        @pl.when(high < levels)
        def _():
            slot = high * GROUP + col
            for part in (2, 0, 1):
                arrive(part, slot)

                @pl.when(has_down)
                def _():
                    push_part(0, part, slot, down_dev)

                push_part(1, part, slot, x_dev)
                push_part(2, part, slot, c_dev)

        @pl.when(low >= 0)
        def _():
            slot = low * GROUP + col
            for part in (2, 0, 1):
                arrive(part, slot)

                @pl.when(has_up)
                def _():
                    push_part(0, part, slot, up_dev)

                push_part(1, part, slot, x_dev)
                push_part(2, part, slot, c_dev)

        before = dist - 1

        @pl.when(level + before < levels)
        def _():
            cross(level + before)

        @pl.when((before > 0) & (level - before >= 0))
        def _():
            cross(level - before)

        return carry

    lax.fori_loop(1, levels + 1, step, 0)

    def finish(other, carry):
        for column in (colc, (colc + 2) % GROUP):
            for part in range(3):
                arrive(part, other * GROUP + column)
        own_slot = other * GROUP + col
        sent(1, own_slot)
        sent(2, own_slot)
        sent(2, other * GROUP + colx)

        @pl.when(has_down & (other >= level))
        def _():
            sent(0, own_slot)

        @pl.when(has_up & (other < level))
        def _():
            sent(0, own_slot)

        @pl.when(has_up & (other == level))
        def _():
            sent(3, own_slot)

        return carry

    lax.fori_loop(0, levels, finish, 0)


def gather(queries, out_grad, keys, values, meta):
    count = lax.axis_size("ctx")
    rows = queries.shape
    anywhere = pl.BlockSpec(memory_space=pl.ANY)
    return pl.pallas_call(
        functools.partial(gather_kernel, count // GROUP),
        out_shape=(
            jax.ShapeDtypeStruct((count,) + rows, queries.dtype),
            jax.ShapeDtypeStruct((count,) + rows, queries.dtype),
            jax.ShapeDtypeStruct((count,) + meta.shape, meta.dtype),
        ),
        in_specs=[anywhere] * 5,
        out_specs=(anywhere,) * 3,
        scratch_shapes=[
            pltpu.SemaphoreType.DMA((4, 3, count)),
            pltpu.SemaphoreType.DMA((3, count)),
        ],
        compiler_params=pltpu.CompilerParams(collective_id=0, has_side_effects=True),
    )(queries, out_grad, keys, values, meta)


def dot(left, right, dims):
    return lax.dot_general(left, right, dims, preferred_element_type=jnp.float32)


def compute_kernel(
    blocks, heads, top, block_len, dh, factor,
    tab_ref, sel_ref,
    q_ref, g_ref, k_ref, v_ref, stat_ref, own_ref, m_buf, a_buf, b_buf,
    dq_ref, dk_ref, dv_ref,
    jq, jg, sk, sv, kacc, vacc, job_src, job_pair, job_key, job_sem, sel_sem,
):
    me = lax.axis_index("ctx")
    count = m_buf.shape[0]
    pairs = blocks * heads
    per_dev = pairs * top
    first = me * blocks

    def where_of(ref, dev, block, head):
        return ref.at[dev, pl.ds(block * block_len, block_len), pl.ds(head * dh, dh)]

    def own_of(ref, block, head):
        return ref.at[pl.ds(block * block_len, block_len), pl.ds(head * dh, dh)]

    for entry in range(per_dev):
        chosen = sel_ref[entry]
        block, head = entry // top // heads, entry // top % heads

        @pl.when(chosen >= 0)
        def _():
            dev, inner = chosen // blocks, chosen % blocks
            pltpu.make_async_copy(where_of(a_buf, dev, inner, head), sk.at[entry], sel_sem.at[0, entry]).start()
            pltpu.make_async_copy(where_of(b_buf, dev, inner, head), sv.at[entry], sel_sem.at[1, entry]).start()

        @pl.when(chosen < 0)
        def _():
            pltpu.make_async_copy(own_of(k_ref, block, head), sk.at[entry], sel_sem.at[0, entry]).start()
            pltpu.make_async_copy(own_of(v_ref, block, head), sv.at[entry], sel_sem.at[1, entry]).start()

    def scan(dev, found):
        for entry in range(per_dev):
            chosen = tab_ref[dev * per_dev + entry]
            block, head = entry // top // heads, entry // top % heads
            hit = (chosen >= first) & (chosen < first + blocks)

            @pl.when(hit)
            def _():
                job_src[found] = dev
                job_pair[found] = entry // top
                job_key[found] = (chosen - first) * heads + head
                pltpu.make_async_copy(where_of(a_buf, dev, block, head), jq.at[found], job_sem.at[0, found]).start()
                pltpu.make_async_copy(where_of(b_buf, dev, block, head), jg.at[found], job_sem.at[1, found]).start()

            found = found + hit.astype(jnp.int32)
        return found

    found = lax.fori_loop(me + 1, count, scan, jnp.int32(0))

    def owner_terms(keys, vals, qs, gs, norm, delta, causal):
        scores = dot(keys, qs, NT) * factor
        weights = jnp.exp(scores - norm)
        if causal:
            at_key = lax.broadcasted_iota(jnp.int32, scores.shape, 0)
            at_query = lax.broadcasted_iota(jnp.int32, scores.shape, 1)
            weights = jnp.where(at_key <= at_query, weights, 0.0)
        dweights = dot(vals, gs, NT)
        dscores = (weights * (dweights - delta)).astype(jnp.bfloat16)
        return dot(dscores, qs, NN) * factor, dot(weights.astype(jnp.bfloat16), gs, NN)

    def piece(ref, block, head):
        return ref[block * block_len:(block + 1) * block_len, head * dh:(head + 1) * dh]

    for pair in range(pairs):
        block, head = pair // heads, pair % heads
        part_k, part_v = owner_terms(
            piece(k_ref, block, head), piece(v_ref, block, head),
            piece(q_ref, block, head), piece(g_ref, block, head),
            own_ref[pair:pair + 1, :], own_ref[pairs + pair:pairs + pair + 1, :], True,
        )
        kacc[pair] = part_k
        vacc[pair] = part_v

    for entry in range(per_dev):
        pltpu.make_async_copy(own_of(k_ref, 0, 0), sk.at[entry], sel_sem.at[0, entry]).wait()
        pltpu.make_async_copy(own_of(v_ref, 0, 0), sv.at[entry], sel_sem.at[1, entry]).wait()
    wide = top * block_len
    for pair in range(pairs):
        block, head = pair // heads, pair % heads
        qs, gs = piece(q_ref, block, head), piece(g_ref, block, head)
        own_k, own_v = piece(k_ref, block, head), piece(v_ref, block, head)
        rows = slice(block * block_len, (block + 1) * block_len)
        norm = stat_ref[rows, head:head + 1]
        delta = stat_ref[rows, heads + head:heads + head + 1]
        far_k = sk[pair * top:(pair + 1) * top].reshape(wide, dh)
        far_v = sv[pair * top:(pair + 1) * top].reshape(wide, dh)
        weights = jnp.exp(dot(qs, own_k, NT) * factor - norm)
        at_query = lax.broadcasted_iota(jnp.int32, weights.shape, 0)
        at_key = lax.broadcasted_iota(jnp.int32, weights.shape, 1)
        weights = jnp.where(at_key <= at_query, weights, 0.0)
        near = (weights * (dot(gs, own_v, NT) - delta)).astype(jnp.bfloat16)
        weights = jnp.exp(dot(qs, far_k, NT) * factor - norm)
        far = weights * (dot(gs, far_v, NT) - delta)
        parts = []
        for turn in range(top):
            part = far[:, turn * block_len:(turn + 1) * block_len]
            parts.append(jnp.where(sel_ref[pair * top + turn] >= 0, part, 0.0))
        far = jnp.concatenate(parts, axis=1).astype(jnp.bfloat16)
        total = (dot(near, own_k, NN) + dot(far, far_k, NN)) * factor
        dq_ref[rows, head * dh:(head + 1) * dh] = total.astype(dq_ref.dtype)

    def drain(job, carry):
        pltpu.make_async_copy(own_of(k_ref, 0, 0), jq.at[job], job_sem.at[0, job]).wait()
        pltpu.make_async_copy(own_of(v_ref, 0, 0), jg.at[job], job_sem.at[1, job]).wait()
        return carry

    lax.fori_loop(0, found, drain, 0)

    def turn(step, carry):
        results = []
        for lane in range(JOBS_STEP):
            job = step * JOBS_STEP + lane
            live = job < found
            job = jnp.minimum(job, found - 1)
            key = job_key[job]
            src, pair = job_src[job], job_pair[job]
            block, head = key // heads, key % heads
            rows = pl.ds(pl.multiple_of(block * block_len, block_len), block_len)
            cols = pl.ds(pl.multiple_of(head * dh, dh), dh)
            part_k, part_v = owner_terms(
                k_ref[rows, cols], v_ref[rows, cols], jq[job], jg[job],
                m_buf[src, pl.ds(pair, 1), :], m_buf[src, pl.ds(pairs + pair, 1), :], False,
            )
            results.append((key, jnp.where(live, part_k, 0.0), jnp.where(live, part_v, 0.0)))
        for key, part_k, part_v in results:
            kacc[key] += part_k
            vacc[key] += part_v
        return carry

    lax.fori_loop(0, (found + JOBS_STEP - 1) // JOBS_STEP, turn, 0)
    for pair in range(pairs):
        block, head = pair // heads, pair % heads
        rows = slice(block * block_len, (block + 1) * block_len)
        dk_ref[rows, head * dh:(head + 1) * dh] = kacc[pair].astype(dk_ref.dtype)
        dv_ref[rows, head * dh:(head + 1) * dh] = vacc[pair].astype(dv_ref.dtype)


def stat_pairs(matrix, blocks):
    row_count, heads = matrix.shape
    shaped = matrix.reshape(blocks, row_count // blocks, heads)
    return jnp.transpose(shaped, (0, 2, 1)).reshape(blocks * heads, row_count // blocks)


def shards(queries, keys, values, out_grad, outputs, log_norms, selected):
    blocks, heads, top = selected.shape
    row_count, width = queries.shape
    dh = width // heads
    block_len = row_count // blocks
    pairs = blocks * heads
    count = lax.axis_size("ctx")
    per_dev = pairs * top
    deltas = jnp.sum(
        (out_grad.astype(jnp.float32) * outputs.astype(jnp.float32)).reshape(row_count, heads, dh), axis=2
    )
    stats = jnp.concatenate([log_norms, deltas], axis=1)
    chosen = selected.reshape(pairs, top).astype(jnp.float32)
    chosen = jnp.pad(chosen, ((0, 0), (0, block_len - top)))
    meta = jnp.concatenate([stat_pairs(log_norms, blocks), stat_pairs(deltas, blocks), chosen], axis=0)
    a_buf, b_buf, m_buf = gather(queries, out_grad, keys, values, meta)
    table = m_buf[:, 2 * pairs:, :top].astype(jnp.int32).reshape(count * per_dev)
    vmem = pl.BlockSpec(memory_space=pltpu.VMEM)
    smem = pl.BlockSpec(memory_space=pltpu.SMEM)
    anywhere = pl.BlockSpec(memory_space=pl.ANY)
    job_max = per_dev * (count - 1) if count < 2 else 2 * count
    grads = jax.ShapeDtypeStruct(queries.shape, jnp.bfloat16)
    grad_q, grad_k, grad_v = pl.pallas_call(
        functools.partial(compute_kernel, blocks, heads, top, block_len, dh, dh ** (-0.5)),
        out_shape=(grads,) * 3,
        in_specs=[smem, smem] + [vmem] * 7 + [anywhere] * 2,
        out_specs=(vmem,) * 3,
        scratch_shapes=[
            pltpu.VMEM((job_max, block_len, dh), jnp.bfloat16),
            pltpu.VMEM((job_max, block_len, dh), jnp.bfloat16),
            pltpu.VMEM((per_dev, block_len, dh), jnp.bfloat16),
            pltpu.VMEM((per_dev, block_len, dh), jnp.bfloat16),
            pltpu.VMEM((pairs, block_len, dh), jnp.float32),
            pltpu.VMEM((pairs, block_len, dh), jnp.float32),
            pltpu.SMEM((job_max,), jnp.int32),
            pltpu.SMEM((job_max,), jnp.int32),
            pltpu.SMEM((job_max,), jnp.int32),
            pltpu.SemaphoreType.DMA((2, job_max)),
            pltpu.SemaphoreType.DMA((2, per_dev)),
        ],
    )(
        table, selected.reshape(per_dev),
        queries, out_grad, keys, values, stats, meta, m_buf, a_buf, b_buf,
    )
    spread_q = lax.all_to_all(grad_q, "head", split_axis=0, concat_axis=1, tiled=True)
    return (spread_q, grad_k, grad_v)


def solution(mesh):
    placed = (P("ctx", "head"),) * 6 + (P("ctx", "head", None),)
    return jax.shard_map(
        shards,
        mesh=mesh,
        in_specs=placed,
        out_specs=(P(("ctx", "head"), None), P("ctx", "head"), P("ctx", "head")),
        check_vma=False,
    )
```

time: 169 us -> 91.1 us (0.54)
  Pallas kernels: 0 us -> 72.2 us
  blocking collectives: 50.6 us -> 8.61 us
  local copies, waits for them, and re-layouts: 40.3 us -> 4.12 us
  waiting for transfers between devices: 30 us -> 0 us
  starting transfers between devices: 23.6 us -> 0 us
  matrix products: 10 us -> 0 us
  other arithmetic: 10.9 us -> 5.04 us
    pallas_call x0 -> x2, Pallas kernels: none -> 72.2 us  [the longest x1 54.9 us: gather(): pl.pallas_call(functools.partial(gather_kernel, count // GROUP), out_shap...]
    all_gather x1 -> x0, blocking collectives: 50.6 us -> none  [shards(): lax.all_gather(selected, 'ctx', axis=0, tiled=True)]
    all_to_all x4 -> x0, waiting for transfers between devices: 30 us -> none  [the longest x1 21.1 us: shards(): lax.all_to_all(partial_value, 'ctx', split_axis=0, concat_axis=0, tiled=T...]
    all_to_all x4 -> x0, starting transfers between devices: 23.6 us -> none  [the longest x1 8.35 us: shards(): lax.all_to_all(partial_value, 'ctx', split_axis=0, concat_axis=0, tiled=T...]
    gather x27 -> x0, local copies, waits for them, and re-layouts: 22.8 us -> none  [the longest x4 8.68 us: owner_turn(): rows_in = arrived[picked]]
    dot_general x34 -> x0, matrix products: 10 us -> none  [the longest x5 1.58 us: pair_grads(): jnp.einsum('nsd,ntd->nst', query_rows, key_rows, preferred_element_type=j...]
    scatter x4 -> x0, local copies, waits for them, and re-layouts: 8.78 us -> none  [owner_turn(): partial_value = partial_value.at[picked].set(rounded)]
    all_to_all x0 -> x1, blocking collectives: none -> 8.61 us  [shards(): lax.all_to_all(grad_q, 'head', split_axis=0, concat_axis=1, tiled=True)]
  transfers between devices with their start and end apart: 4 -> 0, of which waited for: 3 -> 0; matrix products, arithmetic and copies ran while one was open for 8% -> 0% of each run, Pallas kernels for 0% -> 0%
where the time goes in v1:
time: 91.1 us; the launch traced here: 90.7 us
  Pallas kernels  72.2 us (79%)
  blocking collectives  8.61 us (9%)
  other arithmetic  5.04 us (6%)
  local copies, waits for them, and re-layouts  4.12 us (5%)
    pallas_call x1, Pallas kernels, gather(): pl.pallas_call(functools.partial(gather_kernel, count // GROUP), out_shap...  54.9 us
    pallas_call x1, Pallas kernels, shards(): pl.pallas_call(functools.partial(compute_kernel, blocks, heads, top, bloc...  17.3 us
    all_to_all x1, blocking collectives, shards(): lax.all_to_all(grad_q, 'head', split_axis=0, concat_axis=1, tiled=True)  8.61 us

profile of v1, /device:TPU:0, one launch (start us, length us, event | category | flops | bytes accessed | tf_op | source)
XLA Modules:
  0.0 90.7 jit_solution(4784285702688993494)
XLA Ops:
  0.6 0.7 convert_element_type.19
  1.3 0.8 copy.38
  2.1 0.1 copy.41
  2.2 0.7 reshape.38.sel_ref
  2.9 0.8 copy.39
  3.7 1.1 %convert_multiply_fusion = f32[256,512]{1,0:T(8,128)S(1)} fusion(bf16[256,512]{1,0:T(8,128)(2,1)} %param.11, bf16[256,512]{1,0:T(8,128)(2,1)} %g_ref.3), kind=kLoop, calls=%fused_computation | loop fusion | flops 393216 | bytes 1048576 | tf_op jit(solution)/shard_map/mul | solution.py:358
  4.8 0.2 reshape.34
  5.0 0.3 reduce_sum.9
  5.3 0.8 pad_maximum_fusion.stat_ref
  6.1 0.1 copy.36
  6.2 1.3 %select_maximum_fusion.m_ref.own_ref = f32[24,128]{1,0:T(8,128)} fusion(f32[8,3]{1,0:T(8,128)S(1)} %bitcast.20, f32[8,128]{1,0:T(8,128)S(1)} %bitcast.19, f32[8,128]{1,0:T(8,128)} %bitcast.18), kind=kLoop, calls=%fused_computation.3 | loop fusion | flops 12288 | bytes 20576 | tf_op jit(solution)/shard_map/concatenate | solution.py:363
  7.5 54.9 %shard_map.94 = (bf16[16,256,512]{2,1,0:T(8,128)(2,1)}, bf16[16,256,512]{2,1,0:T(8,128)(2,1)}, f32[16,24,128]{2,1,0:T(8,128)}) custom-call(bf16[256,512]{1,0:T(8,128)(2,1)} %q_ref.3, bf16[256,512]{1,0:T(8,128)(2,1)} %g_ref.3, bf16[256,512]{1,0:T(8,128)(2,1)} %k_ref.3, bf16[256,512]{1,0:T(8,128)(2,1)} %v_ref.3, f32[24,128]{1,0:T(8,128)} %select_maximum_fusion.m_ref.own_ref), custom_call_target="tpu_custom_call" | custom-call | tf_op jit(solution)/shard_map/pallas_call | solution.py:181
  62.4 0.8 slice_convert_fusion
  63.3 0.8 reshape.37.tab_ref
  64.0 17.3 %shard_map.95 = (bf16[256,512]{1,0:T(8,128)(2,1)}, bf16[256,512]{1,0:T(8,128)(2,1)}, bf16[256,512]{1,0:T(8,128)(2,1)}) custom-call(s32[384]{0:T(512)} %reshape.37.tab_ref, s32[24]{0:T(128)} %reshape.38.sel_ref, bf16[256,512]{1,0:T(8,128)(2,1)} %q_ref.3, bf16[256,512]{1,0:T(8,128)(2,1)} %g_ref.3, bf16[256,512]{1,0:T(8,128)(2,1)} %k_ref.3, ...), custom_call_target="tpu_custom_call" | custom-call | tf_op jit(solution)/shard_map/pallas_call | solution.py:371
  81.3 8.6 %all_to_all.19 = bf16[2,128,512]{2,1,0:T(8,128)(2,1)S(1)} all-to-all(bf16[2,128,512]{2,1,0:T(8,128)(2,1)} %bitcast.17), channel_id=1, replica_groups=mesh['ctx'=16,'head'=2] {'head'}, dimensions={0} | all-to-all | bytes 524288 | tf_op jit(solution)/shard_map/all_to_all | solution.py:393
  90.0 0.7 copy.42

commit v2 on v1

--- a/solution.py
+++ b/solution.py
@@ -9,6 +9,7 @@
 
 GROUP = 4
 JOBS_STEP = 4
+PER_PEER = 2
 MESH_ID = pl.DeviceIdType.MESH
 NT = (((1,), (1,)), ((), ()))
 NN = (((1,), (0,)), ((), ()))
@@ -70,8 +71,8 @@
     def arrive(part, slot):
         copy(0, part, slot, bufs[part].at[slot], c_dev).wait_recv()
 
-    def sent(way, slot):
-        for part in range(3):
+    def sent(way, slot, which=(0, 1, 2)):
+        for part in which:
             copy(way, part, slot, bufs[part].at[slot], c_dev).wait_send()
 
     @pl.when(has_down)
@@ -97,12 +98,43 @@
     @pl.when(col % 2 == 0)
     def _():
         push(2, me, c_dev, up_own)
+
+    def by_edge(other):
+        skip_low = (level == 0) & (other == 2)
+        skip_high = (level == levels - 1) & (other == levels - 3)
+        return skip_low | skip_high
+
+    def relay_low(other):
+        return (level == 1) & (other == 2)
+
+    def relay_high(other):
+        return (level == levels - 2) & (other == levels - 3)
 
     def cross(other):
         slot = other * GROUP + colx
         for part in (2, 0, 1):
             arrive(part, slot)
+            if part == 0:
+
+                @pl.when(relay_low(other))
+                def _():
+                    push_part(4, part, slot, down_dev)
+
+                @pl.when(relay_high(other))
+                def _():
+                    push_part(4, part, slot, up_dev)
+
             push_part(2, part, slot, c_dev)
+
+    def push_across(part, other, slot):
+        if part == 0:
+
+            @pl.when(jnp.logical_not(by_edge(other)))
+            def _():
+                push_part(1, part, slot, x_dev)
+
+        else:
+            push_part(1, part, slot, x_dev)
 
     def step(dist, carry):
         high = level + dist
@@ -118,7 +150,7 @@
                 def _():
                     push_part(0, part, slot, down_dev)
 
-                push_part(1, part, slot, x_dev)
+                push_across(part, high, slot)
                 push_part(2, part, slot, c_dev)
 
         @pl.when(low >= 0)
@@ -131,7 +163,7 @@
                 def _():
                     push_part(0, part, slot, up_dev)
 
-                push_part(1, part, slot, x_dev)
+                push_across(part, low, slot)
                 push_part(2, part, slot, c_dev)
 
         before = dist - 1
@@ -153,7 +185,16 @@
             for part in range(3):
                 arrive(part, other * GROUP + column)
         own_slot = other * GROUP + col
-        sent(1, own_slot)
+        sent(1, own_slot, (1, 2))
+
+        @pl.when(jnp.logical_not(by_edge(other)))
+        def _():
+            sent(1, own_slot, (0,))
+
+        @pl.when(relay_low(other) | relay_high(other))
+        def _():
+            sent(4, other * GROUP + colx, (0,))
+
         sent(2, own_slot)
         sent(2, other * GROUP + colx)
 
@@ -188,7 +229,7 @@
         in_specs=[anywhere] * 5,
         out_specs=(anywhere,) * 3,
         scratch_shapes=[
-            pltpu.SemaphoreType.DMA((4, 3, count)),
+            pltpu.SemaphoreType.DMA((5, 3, count)),
             pltpu.SemaphoreType.DMA((3, count)),
         ],
         compiler_params=pltpu.CompilerParams(collective_id=0, has_side_effects=True),
@@ -201,10 +242,10 @@
 
 def compute_kernel(
     blocks, heads, top, block_len, dh, factor,
-    tab_ref, sel_ref,
+    sel_ref,
     q_ref, g_ref, k_ref, v_ref, stat_ref, own_ref, m_buf, a_buf, b_buf,
     dq_ref, dk_ref, dv_ref,
-    jq, jg, sk, sv, kacc, vacc, job_src, job_pair, job_key, job_sem, sel_sem,
+    jq, jg, sk, sv, kacc, vacc, tab_ref, job_src, job_pair, job_key, job_sem, sel_sem, tab_sem,
 ):
     me = lax.axis_index("ctx")
     count = m_buf.shape[0]
@@ -218,8 +259,14 @@
     def own_of(ref, block, head):
         return ref.at[pl.ds(block * block_len, block_len), pl.ds(head * dh, dh)]
 
+    def sel_of(entry):
+        return sel_ref[entry % top, entry // top // heads, entry // top % heads]
+
+    fetch_table = pltpu.make_async_copy(m_buf.at[:, pl.ds(2 * pairs, 1), :], tab_ref, tab_sem)
+    fetch_table.start()
+
     for entry in range(per_dev):
-        chosen = sel_ref[entry]
+        chosen = sel_of(entry)
         block, head = entry // top // heads, entry // top % heads
 
         @pl.when(chosen >= 0)
@@ -235,7 +282,7 @@
 
     def scan(dev, found):
         for entry in range(per_dev):
-            chosen = tab_ref[dev * per_dev + entry]
+            chosen = tab_ref[dev, 0, entry].astype(jnp.int32)
             block, head = entry // top // heads, entry // top % heads
             hit = (chosen >= first) & (chosen < first + blocks)
 
@@ -250,6 +297,7 @@
             found = found + hit.astype(jnp.int32)
         return found
 
+    fetch_table.wait()
     found = lax.fori_loop(me + 1, count, scan, jnp.int32(0))
 
     def owner_terms(keys, vals, qs, gs, norm, delta, causal):
@@ -299,7 +347,7 @@
         parts = []
         for turn in range(top):
             part = far[:, turn * block_len:(turn + 1) * block_len]
-            parts.append(jnp.where(sel_ref[pair * top + turn] >= 0, part, 0.0))
+            parts.append(jnp.where(sel_of(pair * top + turn) >= 0, part, 0.0))
         far = jnp.concatenate(parts, axis=1).astype(jnp.bfloat16)
         total = (dot(near, own_k, NN) + dot(far, far_k, NN)) * factor
         dq_ref[rows, head * dh:(head + 1) * dh] = total.astype(dq_ref.dtype)
@@ -340,10 +388,29 @@
         dv_ref[rows, head * dh:(head + 1) * dh] = vacc[pair].astype(dv_ref.dtype)
 
 
-def stat_pairs(matrix, blocks):
-    row_count, heads = matrix.shape
-    shaped = matrix.reshape(blocks, row_count // blocks, heads)
-    return jnp.transpose(shaped, (0, 2, 1)).reshape(blocks * heads, row_count // blocks)
+def prep_kernel(blocks, heads, top, block_len, dh, sel_ref, g_ref, o_ref, n_ref, stat_ref, meta_ref):
+    pairs = blocks * heads
+    lanes = lax.broadcasted_iota(jnp.int32, (block_len, block_len), 1)
+    for block in range(blocks):
+        rows = slice(block * block_len, (block + 1) * block_len)
+        table = jnp.zeros((block_len, block_len), jnp.float32)
+        for head in range(heads):
+            cols = slice(head * dh, (head + 1) * dh)
+            terms = g_ref[rows, cols].astype(jnp.float32) * o_ref[rows, cols].astype(jnp.float32)
+            delta = jnp.sum(terms, axis=1, keepdims=True)
+            table = jnp.where(lanes == heads + head, delta, table)
+        norms = n_ref[:, rows]
+        spread = jnp.concatenate([norms, jnp.zeros((block_len - heads, block_len), jnp.float32)], axis=0)
+        stat_ref[rows, :] = (table + jnp.transpose(spread))[:, :2 * heads]
+        turned = jnp.transpose(table)
+        meta_ref[block * heads:(block + 1) * heads, :] = norms
+        meta_ref[pairs + block * heads:pairs + (block + 1) * heads, :] = turned[heads:2 * heads]
+    lane = lax.broadcasted_iota(jnp.int32, (8, block_len), 1)
+    chosen = jnp.zeros((8, block_len), jnp.int32)
+    for entry in range(pairs * top):
+        value = sel_ref[entry % top, entry // top // heads, entry // top % heads]
+        chosen = jnp.where(lane == entry, value, chosen)
+    meta_ref[2 * pairs:2 * pairs + 8, :] = chosen.astype(jnp.float32)
 
 
 def shards(queries, keys, values, out_grad, outputs, log_norms, selected):
@@ -354,24 +421,26 @@
     pairs = blocks * heads
     count = lax.axis_size("ctx")
     per_dev = pairs * top
-    deltas = jnp.sum(
-        (out_grad.astype(jnp.float32) * outputs.astype(jnp.float32)).reshape(row_count, heads, dh), axis=2
-    )
-    stats = jnp.concatenate([log_norms, deltas], axis=1)
-    chosen = selected.reshape(pairs, top).astype(jnp.float32)
-    chosen = jnp.pad(chosen, ((0, 0), (0, block_len - top)))
-    meta = jnp.concatenate([stat_pairs(log_norms, blocks), stat_pairs(deltas, blocks), chosen], axis=0)
-    a_buf, b_buf, m_buf = gather(queries, out_grad, keys, values, meta)
-    table = m_buf[:, 2 * pairs:, :top].astype(jnp.int32).reshape(count * per_dev)
     vmem = pl.BlockSpec(memory_space=pltpu.VMEM)
     smem = pl.BlockSpec(memory_space=pltpu.SMEM)
     anywhere = pl.BlockSpec(memory_space=pl.ANY)
-    job_max = per_dev * (count - 1) if count < 2 else 2 * count
+    chosen = jnp.transpose(selected, (2, 0, 1))
+    stats, meta = pl.pallas_call(
+        functools.partial(prep_kernel, blocks, heads, top, block_len, dh),
+        out_shape=(
+            jax.ShapeDtypeStruct((row_count, 2 * heads), jnp.float32),
+            jax.ShapeDtypeStruct((2 * pairs + 8, block_len), jnp.float32),
+        ),
+        in_specs=[smem] + [vmem] * 3,
+        out_specs=(vmem,) * 2,
+    )(chosen, out_grad, outputs, jnp.transpose(log_norms))
+    a_buf, b_buf, m_buf = gather(queries, out_grad, keys, values, meta)
+    job_max = PER_PEER * count
     grads = jax.ShapeDtypeStruct(queries.shape, jnp.bfloat16)
     grad_q, grad_k, grad_v = pl.pallas_call(
         functools.partial(compute_kernel, blocks, heads, top, block_len, dh, dh ** (-0.5)),
         out_shape=(grads,) * 3,
-        in_specs=[smem, smem] + [vmem] * 7 + [anywhere] * 2,
+        in_specs=[smem] + [vmem] * 7 + [anywhere] * 2,
         out_specs=(vmem,) * 3,
         scratch_shapes=[
             pltpu.VMEM((job_max, block_len, dh), jnp.bfloat16),
@@ -380,14 +449,16 @@
             pltpu.VMEM((per_dev, block_len, dh), jnp.bfloat16),
             pltpu.VMEM((pairs, block_len, dh), jnp.float32),
             pltpu.VMEM((pairs, block_len, dh), jnp.float32),
+            pltpu.SMEM((count, 1, block_len), jnp.float32),
             pltpu.SMEM((job_max,), jnp.int32),
             pltpu.SMEM((job_max,), jnp.int32),
             pltpu.SMEM((job_max,), jnp.int32),
             pltpu.SemaphoreType.DMA((2, job_max)),
             pltpu.SemaphoreType.DMA((2, per_dev)),
+            pltpu.SemaphoreType.DMA,
         ],
     )(
-        table, selected.reshape(per_dev),
+        chosen,
         queries, out_grad, keys, values, stats, meta, m_buf, a_buf, b_buf,
     )
     spread_q = lax.all_to_all(grad_q, "head", split_axis=0, concat_axis=1, tiled=True)

time: 91.1 us -> 81.4 us (0.89)
  other arithmetic: 5.04 us -> 0 us
  local copies, waits for them, and re-layouts: 4.12 us -> 0.73 us
  Pallas kernels: 72.2 us -> 71.1 us
    pallas_call x1, Pallas kernels: 54.9 us -> 51.2 us  [gather(): pl.pallas_call(functools.partial(gather_kernel, count // GROUP), out_shap...]
    concatenate x2 -> x0, other arithmetic: 2.05 us -> none  [the longest x1 1.3 us: shards(): jnp.concatenate([stat_pairs(log_norms, blocks), stat_pairs(deltas, blocks...]
    pallas_call x0 -> x1, Pallas kernels: none -> 1.99 us  [shards(): pl.pallas_call(functools.partial(prep_kernel, blocks, heads, top, block_l...]
    reshape x4 -> x0, local copies, waits for them, and re-layouts: 1.7 us -> none  [the longest x1 0.79 us: shards(): m_buf[:, 2 * pairs:, :top].astype(jnp.int32).reshape(count * per_dev)]
    unnamed x2 -> x0, local copies, waits for them, and re-layouts: 1.59 us -> none
    convert_element_type x2 -> x0, other arithmetic: 1.54 us -> none  [the longest x1 0.85 us: shards(): m_buf[:, 2 * pairs:, :top].astype(jnp.int32).reshape(count * per_dev)]
    mul x1 -> x0, other arithmetic: 1.1 us -> none  [shards(): out_grad.astype(jnp.float32) * outputs.astype(jnp.float32)]
where the time goes in v2:
time: 81.4 us; the launch traced here: 81.1 us
  Pallas kernels  71.1 us (87%)
  blocking collectives  8.61 us (11%)
    pallas_call x1, Pallas kernels, gather(): pl.pallas_call(functools.partial(gather_kernel, count // GROUP), out_shap...  51.2 us
    pallas_call x1, Pallas kernels, shards(): pl.pallas_call(functools.partial(compute_kernel, blocks, heads, top, bloc...  17.9 us
    all_to_all x1, blocking collectives, shards(): lax.all_to_all(grad_q, 'head', split_axis=0, concat_axis=1, tiled=True)  8.61 us
    pallas_call x1, Pallas kernels, shards(): pl.pallas_call(functools.partial(prep_kernel, blocks, heads, top, block_l...  1.99 us

profile of v2, /device:TPU:0, one launch (start us, length us, event | category | flops | bytes accessed | tf_op | source)
XLA Modules:
  0.0 81.1 jit_solution(16630549925113151240)
XLA Ops:
  0.6 2.0 %shard_map.94 = (f32[256,8]{1,0:T(8,128)}, f32[24,128]{1,0:T(8,128)}) custom-call(s32[3,2,4]{2,1,0:T(2,128)} %bitcast.9, bf16[256,512]{1,0:T(8,128)(2,1)} %g_ref.5, bf16[256,512]{1,0:T(8,128)(2,1)} %o_ref.1, f32[4,256]{1,0:T(4,128)} %bitcast.11), custom_call_target="tpu_custom_call" | custom-call | tf_op jit(solution)/shard_map/pallas_call | solution.py:428
  2.6 51.2 %shard_map.95 = (bf16[16,256,512]{2,1,0:T(8,128)(2,1)}, bf16[16,256,512]{2,1,0:T(8,128)(2,1)}, f32[16,24,128]{2,1,0:T(8,128)}) custom-call(bf16[256,512]{1,0:T(8,128)(2,1)} %q_ref.3, bf16[256,512]{1,0:T(8,128)(2,1)} %g_ref.5, bf16[256,512]{1,0:T(8,128)(2,1)} %k_ref.3, bf16[256,512]{1,0:T(8,128)(2,1)} %v_ref.3, f32[24,128]{1,0:T(8,128)} %get-tuple-element.12.m_ref.own_ref), custom_call_target="tpu_custom_call" | custom-call | tf_op jit(solution)/shard_map/pallas_call | solution.py:222
  53.8 17.9 %shard_map.96 = (bf16[256,512]{1,0:T(8,128)(2,1)}, bf16[256,512]{1,0:T(8,128)(2,1)}, bf16[256,512]{1,0:T(8,128)(2,1)}) custom-call(s32[3,2,4]{2,1,0:T(2,128)} %bitcast.10, bf16[256,512]{1,0:T(8,128)(2,1)} %q_ref.3, bf16[256,512]{1,0:T(8,128)(2,1)} %g_ref.5, bf16[256,512]{1,0:T(8,128)(2,1)} %k_ref.3, bf16[256,512]{1,0:T(8,128)(2,1)} %v_ref.3, ...), custom_call_target="tpu_custom_call" | custom-call | tf_op jit(solution)/shard_map/pallas_call | solution.py:440
  71.8 8.6 %all_to_all.19 = bf16[2,128,512]{2,1,0:T(8,128)(2,1)S(1)} all-to-all(bf16[2,128,512]{2,1,0:T(8,128)(2,1)} %bitcast.8), channel_id=1, replica_groups=mesh['ctx'=16,'head'=2] {'head'}, dimensions={0} | all-to-all | bytes 524288 | tf_op jit(solution)/shard_map/all_to_all | solution.py:464
  80.4 0.7 copy.11

commit v3 on v2

--- a/solution.py
+++ b/solution.py
@@ -240,30 +240,30 @@
     return lax.dot_general(left, right, dims, preferred_element_type=jnp.float32)
 
 
-def compute_kernel(
+def piece(ref, block, head, block_len, dh):
+    return ref[block * block_len:(block + 1) * block_len, head * dh:(head + 1) * dh]
+
+
+def view(ref, block, head, block_len, dh):
+    return ref.at[pl.ds(block * block_len, block_len), pl.ds(head * dh, dh)]
+
+
+def far_view(ref, dev, block, head, block_len, dh):
+    return ref.at[dev, pl.ds(block * block_len, block_len), pl.ds(head * dh, dh)]
+
+
+def query_kernel(
     blocks, heads, top, block_len, dh, factor,
-    sel_ref,
-    q_ref, g_ref, k_ref, v_ref, stat_ref, own_ref, m_buf, a_buf, b_buf,
-    dq_ref, dk_ref, dv_ref,
-    jq, jg, sk, sv, kacc, vacc, tab_ref, job_src, job_pair, job_key, job_sem, sel_sem, tab_sem,
+    sel_ref, q_ref, g_ref, k_ref, v_ref, stat_ref, a_buf, b_buf, dq_ref, sk, sv, sel_sem,
 ):
-    me = lax.axis_index("ctx")
-    count = m_buf.shape[0]
+    chunks, size = dq_ref.shape[0], dq_ref.shape[1]
+    mine = lax.axis_index("head")
     pairs = blocks * heads
     per_dev = pairs * top
-    first = me * blocks
-
-    def where_of(ref, dev, block, head):
-        return ref.at[dev, pl.ds(block * block_len, block_len), pl.ds(head * dh, dh)]
-
-    def own_of(ref, block, head):
-        return ref.at[pl.ds(block * block_len, block_len), pl.ds(head * dh, dh)]
+    place = (block_len, dh)
 
     def sel_of(entry):
         return sel_ref[entry % top, entry // top // heads, entry // top % heads]
-
-    fetch_table = pltpu.make_async_copy(m_buf.at[:, pl.ds(2 * pairs, 1), :], tab_ref, tab_sem)
-    fetch_table.start()
 
     for entry in range(per_dev):
         chosen = sel_of(entry)
@@ -272,66 +272,22 @@
         @pl.when(chosen >= 0)
         def _():
             dev, inner = chosen // blocks, chosen % blocks
-            pltpu.make_async_copy(where_of(a_buf, dev, inner, head), sk.at[entry], sel_sem.at[0, entry]).start()
-            pltpu.make_async_copy(where_of(b_buf, dev, inner, head), sv.at[entry], sel_sem.at[1, entry]).start()
+            pltpu.make_async_copy(far_view(a_buf, dev, inner, head, *place), sk.at[entry], sel_sem.at[0, entry]).start()
+            pltpu.make_async_copy(far_view(b_buf, dev, inner, head, *place), sv.at[entry], sel_sem.at[1, entry]).start()
 
         @pl.when(chosen < 0)
         def _():
-            pltpu.make_async_copy(own_of(k_ref, block, head), sk.at[entry], sel_sem.at[0, entry]).start()
-            pltpu.make_async_copy(own_of(v_ref, block, head), sv.at[entry], sel_sem.at[1, entry]).start()
-
-    def scan(dev, found):
-        for entry in range(per_dev):
-            chosen = tab_ref[dev, 0, entry].astype(jnp.int32)
-            block, head = entry // top // heads, entry // top % heads
-            hit = (chosen >= first) & (chosen < first + blocks)
-
-            @pl.when(hit)
-            def _():
-                job_src[found] = dev
-                job_pair[found] = entry // top
-                job_key[found] = (chosen - first) * heads + head
-                pltpu.make_async_copy(where_of(a_buf, dev, block, head), jq.at[found], job_sem.at[0, found]).start()
-                pltpu.make_async_copy(where_of(b_buf, dev, block, head), jg.at[found], job_sem.at[1, found]).start()
-
-            found = found + hit.astype(jnp.int32)
-        return found
-
-    fetch_table.wait()
-    found = lax.fori_loop(me + 1, count, scan, jnp.int32(0))
-
-    def owner_terms(keys, vals, qs, gs, norm, delta, causal):
-        scores = dot(keys, qs, NT) * factor
-        weights = jnp.exp(scores - norm)
-        if causal:
-            at_key = lax.broadcasted_iota(jnp.int32, scores.shape, 0)
-            at_query = lax.broadcasted_iota(jnp.int32, scores.shape, 1)
-            weights = jnp.where(at_key <= at_query, weights, 0.0)
-        dweights = dot(vals, gs, NT)
-        dscores = (weights * (dweights - delta)).astype(jnp.bfloat16)
-        return dot(dscores, qs, NN) * factor, dot(weights.astype(jnp.bfloat16), gs, NN)
-
-    def piece(ref, block, head):
-        return ref[block * block_len:(block + 1) * block_len, head * dh:(head + 1) * dh]
-
-    for pair in range(pairs):
-        block, head = pair // heads, pair % heads
-        part_k, part_v = owner_terms(
-            piece(k_ref, block, head), piece(v_ref, block, head),
-            piece(q_ref, block, head), piece(g_ref, block, head),
-            own_ref[pair:pair + 1, :], own_ref[pairs + pair:pairs + pair + 1, :], True,
-        )
-        kacc[pair] = part_k
-        vacc[pair] = part_v
+            pltpu.make_async_copy(view(k_ref, block, head, *place), sk.at[entry], sel_sem.at[0, entry]).start()
+            pltpu.make_async_copy(view(v_ref, block, head, *place), sv.at[entry], sel_sem.at[1, entry]).start()
 
     for entry in range(per_dev):
-        pltpu.make_async_copy(own_of(k_ref, 0, 0), sk.at[entry], sel_sem.at[0, entry]).wait()
-        pltpu.make_async_copy(own_of(v_ref, 0, 0), sv.at[entry], sel_sem.at[1, entry]).wait()
+        pltpu.make_async_copy(view(k_ref, 0, 0, *place), sk.at[entry], sel_sem.at[0, entry]).wait()
+        pltpu.make_async_copy(view(v_ref, 0, 0, *place), sv.at[entry], sel_sem.at[1, entry]).wait()
     wide = top * block_len
     for pair in range(pairs):
         block, head = pair // heads, pair % heads
-        qs, gs = piece(q_ref, block, head), piece(g_ref, block, head)
-        own_k, own_v = piece(k_ref, block, head), piece(v_ref, block, head)
+        qs, gs = piece(q_ref, block, head, *place), piece(g_ref, block, head, *place)
+        own_k, own_v = piece(k_ref, block, head, *place), piece(v_ref, block, head, *place)
         rows = slice(block * block_len, (block + 1) * block_len)
         norm = stat_ref[rows, head:head + 1]
         delta = stat_ref[rows, heads + head:heads + head + 1]
@@ -349,12 +305,75 @@
             part = far[:, turn * block_len:(turn + 1) * block_len]
             parts.append(jnp.where(sel_of(pair * top + turn) >= 0, part, 0.0))
         far = jnp.concatenate(parts, axis=1).astype(jnp.bfloat16)
-        total = (dot(near, own_k, NN) + dot(far, far_k, NN)) * factor
-        dq_ref[rows, head * dh:(head + 1) * dh] = total.astype(dq_ref.dtype)
+        total = ((dot(near, own_k, NN) + dot(far, far_k, NN)) * factor).astype(dq_ref.dtype)
+        step = min(size, block_len)
+        for start in range(0, block_len, step):
+            row = block * block_len + start
+            chunk = (row // size + chunks - mine) % chunks
+            dq_ref[chunk, row % size:row % size + step, head * dh:(head + 1) * dh] = total[start:start + step]
+
+
+def owner_kernel(
+    blocks, heads, block_len, dh, factor,
+    q_ref, g_ref, k_ref, v_ref, own_ref, m_buf, a_buf, b_buf,
+    dk_ref, dv_ref,
+    jq, jg, kacc, vacc, tab_ref, job_src, job_pair, job_key, job_sem, tab_sem,
+):
+    me = lax.axis_index("ctx")
+    count = m_buf.shape[0]
+    pairs = blocks * heads
+    place = (block_len, dh)
+
+    fetch_table = pltpu.make_async_copy(m_buf.at[:, pl.ds(2 * pairs, PER_PEER), :], tab_ref, tab_sem)
+    fetch_table.start()
+    fetch_table.wait()
+
+    def scan(dev, found):
+        for rank in range(PER_PEER):
+            code = tab_ref[dev, rank, me].astype(jnp.int32)
+            pair = code // blocks
+            block, head = pair // heads, pair % heads
+
+            @pl.when(code >= 0)
+            def _():
+                job_src[found] = dev
+                job_pair[found] = pair
+                job_key[found] = (code % blocks) * heads + head
+                row = pl.multiple_of(block * block_len, block_len)
+                col = pl.multiple_of(head * dh, dh)
+                spot = (dev, pl.ds(row, block_len), pl.ds(col, dh))
+                pltpu.make_async_copy(a_buf.at[spot], jq.at[found], job_sem.at[0, found]).start()
+                pltpu.make_async_copy(b_buf.at[spot], jg.at[found], job_sem.at[1, found]).start()
+
+            found = found + (code >= 0).astype(jnp.int32)
+        return found
+
+    found = lax.fori_loop(me + 1, count, scan, jnp.int32(0))
+
+    def owner_terms(keys, vals, qs, gs, norm, delta, causal):
+        scores = dot(keys, qs, NT) * factor
+        weights = jnp.exp(scores - norm)
+        if causal:
+            at_key = lax.broadcasted_iota(jnp.int32, scores.shape, 0)
+            at_query = lax.broadcasted_iota(jnp.int32, scores.shape, 1)
+            weights = jnp.where(at_key <= at_query, weights, 0.0)
+        dweights = dot(vals, gs, NT)
+        dscores = (weights * (dweights - delta)).astype(jnp.bfloat16)
+        return dot(dscores, qs, NN) * factor, dot(weights.astype(jnp.bfloat16), gs, NN)
+
+    for pair in range(pairs):
+        block, head = pair // heads, pair % heads
+        part_k, part_v = owner_terms(
+            piece(k_ref, block, head, *place), piece(v_ref, block, head, *place),
+            piece(q_ref, block, head, *place), piece(g_ref, block, head, *place),
+            own_ref[pair:pair + 1, :], own_ref[pairs + pair:pairs + pair + 1, :], True,
+        )
+        kacc[pair] = part_k
+        vacc[pair] = part_v
 
     def drain(job, carry):
-        pltpu.make_async_copy(own_of(k_ref, 0, 0), jq.at[job], job_sem.at[0, job]).wait()
-        pltpu.make_async_copy(own_of(v_ref, 0, 0), jg.at[job], job_sem.at[1, job]).wait()
+        pltpu.make_async_copy(view(k_ref, 0, 0, *place), jq.at[job], job_sem.at[0, job]).wait()
+        pltpu.make_async_copy(view(v_ref, 0, 0, *place), jg.at[job], job_sem.at[1, job]).wait()
         return carry
 
     lax.fori_loop(0, found, drain, 0)
@@ -388,6 +407,16 @@
         dv_ref[rows, head * dh:(head + 1) * dh] = vacc[pair].astype(dv_ref.dtype)
 
 
+def join_kernel(chunk_ref, *refs):
+    moved, out_ref = refs[:-1], refs[-1]
+    chunks, size, width = chunk_ref.shape
+    mine = lax.axis_index("head")
+    for shift in range(chunks):
+        source = (mine + chunks - shift) % chunks
+        cols = pl.ds(pl.multiple_of(source * width, width), width)
+        out_ref[:, cols] = chunk_ref[0] if shift == 0 else moved[shift - 1][...]
+
+
 def prep_kernel(blocks, heads, top, block_len, dh, sel_ref, g_ref, o_ref, n_ref, stat_ref, meta_ref):
     pairs = blocks * heads
     lanes = lax.broadcasted_iota(jnp.int32, (block_len, block_len), 1)
@@ -406,11 +435,21 @@
         meta_ref[block * heads:(block + 1) * heads, :] = norms
         meta_ref[pairs + block * heads:pairs + (block + 1) * heads, :] = turned[heads:2 * heads]
     lane = lax.broadcasted_iota(jnp.int32, (8, block_len), 1)
-    chosen = jnp.zeros((8, block_len), jnp.int32)
+    slots = [jnp.full((8, block_len), -1, jnp.int32) for _ in range(PER_PEER)]
     for entry in range(pairs * top):
         value = sel_ref[entry % top, entry // top // heads, entry // top % heads]
-        chosen = jnp.where(lane == entry, value, chosen)
-    meta_ref[2 * pairs:2 * pairs + 8, :] = chosen.astype(jnp.float32)
+        owner = jnp.where(value >= 0, value // blocks, -1)
+        code = (entry // top) * blocks + value % blocks
+        here = lane == owner
+        for rank in range(PER_PEER):
+            free = slots[rank] < 0
+            slots[rank] = jnp.where(here & free, code, slots[rank])
+            here = here & jnp.logical_not(free)
+    row = lax.broadcasted_iota(jnp.int32, (8, block_len), 0)
+    table = jnp.zeros((8, block_len), jnp.int32)
+    for rank in range(PER_PEER):
+        table = jnp.where(row == rank, slots[rank], table)
+    meta_ref[2 * pairs:2 * pairs + 8, :] = table.astype(jnp.float32)
 
 
 def shards(queries, keys, values, out_grad, outputs, log_norms, selected):
@@ -436,32 +475,46 @@
     )(chosen, out_grad, outputs, jnp.transpose(log_norms))
     a_buf, b_buf, m_buf = gather(queries, out_grad, keys, values, meta)
     job_max = PER_PEER * count
+    chunks = lax.axis_size("head")
+    factor = dh ** (-0.5)
+    spare = pltpu.VMEM((per_dev, block_len, dh), jnp.bfloat16)
+    chunk_q = pl.pallas_call(
+        functools.partial(query_kernel, blocks, heads, top, block_len, dh, factor),
+        out_shape=jax.ShapeDtypeStruct((chunks, row_count // chunks, width), jnp.bfloat16),
+        in_specs=[smem] + [vmem] * 5 + [anywhere] * 2,
+        out_specs=vmem,
+        scratch_shapes=[spare, spare, pltpu.SemaphoreType.DMA((2, per_dev))],
+        cost_estimate=pl.CostEstimate(flops=10**9, bytes_accessed=4 * 10**6, transcendentals=10**6),
+    )(chosen, queries, out_grad, keys, values, stats, a_buf, b_buf)
+    moved = []
+    for shift in range(1, chunks):
+        ring = [(at, (at + shift) % chunks) for at in range(chunks)]
+        moved.append(lax.ppermute(chunk_q[shift], "head", ring))
     grads = jax.ShapeDtypeStruct(queries.shape, jnp.bfloat16)
-    grad_q, grad_k, grad_v = pl.pallas_call(
-        functools.partial(compute_kernel, blocks, heads, top, block_len, dh, dh ** (-0.5)),
-        out_shape=(grads,) * 3,
-        in_specs=[smem] + [vmem] * 7 + [anywhere] * 2,
-        out_specs=(vmem,) * 3,
+    jobs = pltpu.VMEM((job_max, block_len, dh), jnp.bfloat16)
+    sums = pltpu.VMEM((pairs, block_len, dh), jnp.float32)
+    grad_k, grad_v = pl.pallas_call(
+        functools.partial(owner_kernel, blocks, heads, block_len, dh, factor),
+        out_shape=(grads,) * 2,
+        in_specs=[vmem] * 6 + [anywhere] * 2,
+        out_specs=(vmem,) * 2,
         scratch_shapes=[
-            pltpu.VMEM((job_max, block_len, dh), jnp.bfloat16),
-            pltpu.VMEM((job_max, block_len, dh), jnp.bfloat16),
-            pltpu.VMEM((per_dev, block_len, dh), jnp.bfloat16),
-            pltpu.VMEM((per_dev, block_len, dh), jnp.bfloat16),
-            pltpu.VMEM((pairs, block_len, dh), jnp.float32),
-            pltpu.VMEM((pairs, block_len, dh), jnp.float32),
-            pltpu.SMEM((count, 1, block_len), jnp.float32),
+            jobs, jobs, sums, sums,
+            pltpu.SMEM((count, PER_PEER, block_len), jnp.float32),
             pltpu.SMEM((job_max,), jnp.int32),
             pltpu.SMEM((job_max,), jnp.int32),
             pltpu.SMEM((job_max,), jnp.int32),
             pltpu.SemaphoreType.DMA((2, job_max)),
-            pltpu.SemaphoreType.DMA((2, per_dev)),
             pltpu.SemaphoreType.DMA,
         ],
-    )(
-        chosen,
-        queries, out_grad, keys, values, stats, meta, m_buf, a_buf, b_buf,
-    )
-    spread_q = lax.all_to_all(grad_q, "head", split_axis=0, concat_axis=1, tiled=True)
+        cost_estimate=pl.CostEstimate(flops=4 * 10**9, bytes_accessed=8 * 10**6, transcendentals=10**6),
+    )(queries, out_grad, keys, values, meta, m_buf, a_buf, b_buf)
+    spread_q = pl.pallas_call(
+        join_kernel,
+        out_shape=jax.ShapeDtypeStruct((row_count // chunks, chunks * width), jnp.bfloat16),
+        in_specs=[vmem] * chunks,
+        out_specs=vmem,
+    )(chunk_q, *moved)
     return (spread_q, grad_k, grad_v)
 
 

time: 81.4 us -> 78.2 us (0.961); the launches traced: 81.1 us -> 76.7 us
  blocking collectives: 8.61 us -> 0 us
  Pallas kernels: 71.1 us -> 72.8 us
  starting transfers between devices: 0 us -> 1.58 us
  local copies, waits for them, and re-layouts: 0.73 us -> 1.56 us
    all_to_all x1 -> x0, blocking collectives: 8.61 us -> none  [shards(): lax.all_to_all(grad_q, 'head', split_axis=0, concat_axis=1, tiled=True)]
    pallas_call x1 -> x3, Pallas kernels: 17.9 us -> 19.6 us  [the longest x1 12.7 us: shards(): pl.pallas_call(functools.partial(owner_kernel, blocks, heads, block_len,...]
    ppermute x0 -> x1, starting transfers between devices: none -> 1.58 us  [shards(): moved.append(lax.ppermute(chunk_q[shift], 'head', ring))]
    squeeze x0 -> x1, local copies, waits for them, and re-layouts: none -> 0.91 us  [shards(): moved.append(lax.ppermute(chunk_q[shift], 'head', ring))]
  transfers between devices with their start and end apart: 0 -> 1, of which waited for: 0 -> 0; matrix products, arithmetic and copies ran while one was open for 0% -> 0% of each run, Pallas kernels for 0% -> 17%
where the time goes in v3:
time: 78.2 us; the launch traced here: 76.7 us
  Pallas kernels  72.8 us (93%)
  starting transfers between devices  1.58 us (2%)
  local copies, waits for them, and re-layouts  1.56 us (2%)
    pallas_call x1, Pallas kernels, gather(): pl.pallas_call(functools.partial(gather_kernel, count // GROUP), out_shap...  51.2 us
    pallas_call x1, Pallas kernels, shards(): pl.pallas_call(functools.partial(owner_kernel, blocks, heads, block_len,...  12.7 us
    pallas_call x1, Pallas kernels, shards(): pl.pallas_call(functools.partial(query_kernel, blocks, heads, top, block_...  5.23 us
    pallas_call x1, Pallas kernels, shards(): pl.pallas_call(functools.partial(prep_kernel, blocks, heads, top, block_l...  1.99 us
    pallas_call x1, Pallas kernels, shards(): pl.pallas_call(join_kernel, out_shape=jax.ShapeDtypeStruct((row_count //...  1.71 us
    ppermute x1, starting transfers between devices, shards(): moved.append(lax.ppermute(chunk_q[shift], 'head', ring))  1.58 us
  transfers between devices with their start and end apart: 1, of which 0 were waited for; matrix products, arithmetic and copies ran while one was open for 0% of the time, Pallas kernels for 17%

profile of v3, /device:TPU:0, one launch (start us, length us, event | category | flops | bytes accessed | tf_op | source)
XLA Modules:
  0.0 76.7 jit_solution(3519873051757912596)
XLA Ops:
  0.6 2.0 %shard_map.94 = (f32[256,8]{1,0:T(8,128)}, f32[24,128]{1,0:T(8,128)}) custom-call(s32[3,2,4]{2,1,0:T(2,128)} %bitcast.4, bf16[256,512]{1,0:T(8,128)(2,1)} %g_ref.7, bf16[256,512]{1,0:T(8,128)(2,1)} %o_ref.1, f32[4,256]{1,0:T(4,128)} %bitcast.6), custom_call_target="tpu_custom_call" | custom-call | tf_op jit(solution)/shard_map/pallas_call | solution.py:467
  2.6 51.2 %shard_map.95 = (bf16[16,256,512]{2,1,0:T(8,128)(2,1)}, bf16[16,256,512]{2,1,0:T(8,128)(2,1)}, f32[16,24,128]{2,1,0:T(8,128)}) custom-call(bf16[256,512]{1,0:T(8,128)(2,1)} %q_ref.5, bf16[256,512]{1,0:T(8,128)(2,1)} %g_ref.7, bf16[256,512]{1,0:T(8,128)(2,1)} %k_ref.5, bf16[256,512]{1,0:T(8,128)(2,1)} %v_ref.5, f32[24,128]{1,0:T(8,128)} %get-tuple-element.11.m_ref.own_ref), custom_call_target="tpu_custom_call" | custom-call | tf_op jit(solution)/shard_map/pallas_call | solution.py:222
  53.8 5.2 %shard_map.96.chunk_ref = bf16[2,128,512]{2,1,0:T(8,128)(2,1)} custom-call(s32[3,2,4]{2,1,0:T(2,128)} %bitcast.5, bf16[256,512]{1,0:T(8,128)(2,1)} %q_ref.5, bf16[256,512]{1,0:T(8,128)(2,1)} %g_ref.7, bf16[256,512]{1,0:T(8,128)(2,1)} %k_ref.5, bf16[256,512]{1,0:T(8,128)(2,1)} %v_ref.5, f32[256,8]{1,0:T(8,128)} %get-tuple-element.10.stat_ref, ...), custom_call_target="tpu_custom_call" | custom-call | flops 1000000000 | bytes 4000000 | tf_op jit(solution)/shard_map/pallas_call | solution.py:481
  59.1 0.9 %slice_bitcast_fusion = bf16[128,512]{1,0:T(8,128)(2,1)S(1)} fusion(bf16[2,128,512]{2,1,0:T(8,128)(2,1)} %shard_map.96.chunk_ref), kind=kLoop, calls=%fused_computation | loop fusion | bytes 262144 | tf_op jit(solution)/shard_map/squeeze | solution.py:492
  60.0 1.6 %collective-permute-start = (bf16[128,512]{1,0:T(8,128)(2,1)S(1)}, bf16[128,512]{1,0:T(8,128)(2,1)S(1)}, u32[]{:S(2)}, u32[]{:S(2)}) collective-permute-start(bf16[128,512]{1,0:T(8,128)(2,1)S(1)} %slice_bitcast_fusion), channel_id=1, source_target_pairs={{0,1},{1,0},{2,3},{3,2},{4,5},{5,4},{6,7},{7,6},{8,9},{9,8},{10,11... | collective-permute-start | bytes 393224 | tf_op jit(solution)/shard_map/ppermute | solution.py:492
  61.6 12.7 %shard_map.98 = (bf16[256,512]{1,0:T(8,128)(2,1)}, bf16[256,512]{1,0:T(8,128)(2,1)}) custom-call(bf16[256,512]{1,0:T(8,128)(2,1)} %q_ref.5, bf16[256,512]{1,0:T(8,128)(2,1)} %g_ref.7, bf16[256,512]{1,0:T(8,128)(2,1)} %k_ref.5, bf16[256,512]{1,0:T(8,128)(2,1)} %v_ref.5, f32[24,128]{1,0:T(8,128)} %get-tuple-element.11.m_ref.own_ref, ...), custom_call_target="tpu_custom_call" | custom-call | flops 4000000000 | bytes 8000000 | tf_op jit(solution)/shard_map/pallas_call | solution.py:496
  74.3 0.0 collective-permute-done.refs_0_
  74.3 0.0 copy-start
  74.3 0.6 copy-done
  74.9 1.7 %shard_map.97 = bf16[128,1024]{1,0:T(8,128)(2,1)} custom-call(bf16[2,128,512]{2,1,0:T(8,128)(2,1)} %shard_map.96.chunk_ref, bf16[128,512]{1,0:T(8,128)(2,1)} %copy-done), custom_call_target="tpu_custom_call" | custom-call | tf_op jit(solution)/shard_map/pallas_call | solution.py:512
Async XLA Ops:
  60.0 14.3 %collective-permute-start = (bf16[128,512]{1,0:T(8,128)(2,1)S(1)}, bf16[128,512]{1,0:T(8,128)(2,1)S(1)}, u32[]{:S(2)}, u32[]{:S(2)}) collective-permute-start(bf16[128,512]{1,0:T(8,128)(2,1)S(1)} %slice_bitcast_fusion), channel_id=1, source_target_pairs={{0,1},{1,0},{2,3},{3,2},{4,5},{5,4},{6,7},{7,6},{8,9},{9,8},{10,11... | collective-permute-start | bytes 393224 | tf_op jit(solution)/shard_map/ppermute | solution.py:492
  74.3 0.7 copy-start

commit v4 on v3

--- a/solution.py
+++ b/solution.py
@@ -100,15 +100,17 @@
         push(2, me, c_dev, up_own)
 
     def by_edge(other):
-        skip_low = (level == 0) & (other == 2)
-        skip_high = (level == levels - 1) & (other == levels - 3)
-        return skip_low | skip_high
+        to_low = (other == level + 1) | ((level == levels - 1) & (other == levels - 3))
+        to_high = (other == level - 1) | ((level == 0) & (other == 2))
+        return ((col >= 2) & to_low) | ((col < 2) & to_high)
 
     def relay_low(other):
-        return (level == 1) & (other == 2)
+        near = (other == level) & (col < 2) & has_down
+        return near | ((level == 1) & (other == 2) & (col >= 2))
 
     def relay_high(other):
-        return (level == levels - 2) & (other == levels - 3)
+        near = (other == level) & (col >= 2) & has_up
+        return near | ((level == levels - 2) & (other == levels - 3) & (col < 2))
 
     def cross(other):
         slot = other * GROUP + colx

time: 78.2 us -> 79.5 us (1.017); the launches traced: 76.7 us -> 78.8 us
  Pallas kernels: 72.8 us -> 75 us
    pallas_call x1, Pallas kernels: 51.2 us -> 53.4 us  [gather(): pl.pallas_call(functools.partial(gather_kernel, count // GROUP), out_shap...]
  transfers between devices with their start and end apart: 1 -> 1, of which waited for: 0 -> 0; matrix products, arithmetic and copies ran while one was open for 0% -> 0% of each run, Pallas kernels for 17% -> 16%
where the time goes in v4:
time: 79.5 us; the launch traced here: 78.8 us
  Pallas kernels  75 us (94%)
  starting transfers between devices  1.59 us (2%)
  local copies, waits for them, and re-layouts  1.56 us (2%)
    pallas_call x1, Pallas kernels, gather(): pl.pallas_call(functools.partial(gather_kernel, count // GROUP), out_shap...  53.4 us
    pallas_call x1, Pallas kernels, shards(): pl.pallas_call(functools.partial(owner_kernel, blocks, heads, block_len,...  12.7 us
    pallas_call x1, Pallas kernels, shards(): pl.pallas_call(functools.partial(query_kernel, blocks, heads, top, block_...  5.23 us
    pallas_call x1, Pallas kernels, shards(): pl.pallas_call(functools.partial(prep_kernel, blocks, heads, top, block_l...  1.99 us
    pallas_call x1, Pallas kernels, shards(): pl.pallas_call(join_kernel, out_shape=jax.ShapeDtypeStruct((row_count //...  1.71 us
  transfers between devices with their start and end apart: 1, of which 0 were waited for; matrix products, arithmetic and copies ran while one was open for 0% of the time, Pallas kernels for 16%

profile of v4, /device:TPU:0, one launch (start us, length us, event | category | flops | bytes accessed | tf_op | source)
XLA Modules:
  0.0 78.8 jit_solution(12177712021494220028)
XLA Ops:
  0.6 2.0 %shard_map.94 = (f32[256,8]{1,0:T(8,128)}, f32[24,128]{1,0:T(8,128)}) custom-call(s32[3,2,4]{2,1,0:T(2,128)} %bitcast.4, bf16[256,512]{1,0:T(8,128)(2,1)} %g_ref.7, bf16[256,512]{1,0:T(8,128)(2,1)} %o_ref.1, f32[4,256]{1,0:T(4,128)} %bitcast.6), custom_call_target="tpu_custom_call" | custom-call | tf_op jit(solution)/shard_map/pallas_call | solution.py:469
  2.6 53.4 %shard_map.95 = (bf16[16,256,512]{2,1,0:T(8,128)(2,1)}, bf16[16,256,512]{2,1,0:T(8,128)(2,1)}, f32[16,24,128]{2,1,0:T(8,128)}) custom-call(bf16[256,512]{1,0:T(8,128)(2,1)} %q_ref.5, bf16[256,512]{1,0:T(8,128)(2,1)} %g_ref.7, bf16[256,512]{1,0:T(8,128)(2,1)} %k_ref.5, bf16[256,512]{1,0:T(8,128)(2,1)} %v_ref.5, f32[24,128]{1,0:T(8,128)} %get-tuple-element.11.m_ref.own_ref), custom_call_target="tpu_custom_call" | custom-call | tf_op jit(solution)/shard_map/pallas_call | solution.py:224
  56.0 5.2 %shard_map.96.chunk_ref = bf16[2,128,512]{2,1,0:T(8,128)(2,1)} custom-call(s32[3,2,4]{2,1,0:T(2,128)} %bitcast.5, bf16[256,512]{1,0:T(8,128)(2,1)} %q_ref.5, bf16[256,512]{1,0:T(8,128)(2,1)} %g_ref.7, bf16[256,512]{1,0:T(8,128)(2,1)} %k_ref.5, bf16[256,512]{1,0:T(8,128)(2,1)} %v_ref.5, f32[256,8]{1,0:T(8,128)} %get-tuple-element.10.stat_ref, ...), custom_call_target="tpu_custom_call" | custom-call | flops 1000000000 | bytes 4000000 | tf_op jit(solution)/shard_map/pallas_call | solution.py:483
  61.3 0.9 %slice_bitcast_fusion = bf16[128,512]{1,0:T(8,128)(2,1)S(1)} fusion(bf16[2,128,512]{2,1,0:T(8,128)(2,1)} %shard_map.96.chunk_ref), kind=kLoop, calls=%fused_computation | loop fusion | bytes 262144 | tf_op jit(solution)/shard_map/squeeze | solution.py:494
  62.2 1.6 %collective-permute-start = (bf16[128,512]{1,0:T(8,128)(2,1)S(1)}, bf16[128,512]{1,0:T(8,128)(2,1)S(1)}, u32[]{:S(2)}, u32[]{:S(2)}) collective-permute-start(bf16[128,512]{1,0:T(8,128)(2,1)S(1)} %slice_bitcast_fusion), channel_id=1, source_target_pairs={{0,1},{1,0},{2,3},{3,2},{4,5},{5,4},{6,7},{7,6},{8,9},{9,8},{10,11... | collective-permute-start | bytes 393224 | tf_op jit(solution)/shard_map/ppermute | solution.py:494
  63.8 12.7 %shard_map.98 = (bf16[256,512]{1,0:T(8,128)(2,1)}, bf16[256,512]{1,0:T(8,128)(2,1)}) custom-call(bf16[256,512]{1,0:T(8,128)(2,1)} %q_ref.5, bf16[256,512]{1,0:T(8,128)(2,1)} %g_ref.7, bf16[256,512]{1,0:T(8,128)(2,1)} %k_ref.5, bf16[256,512]{1,0:T(8,128)(2,1)} %v_ref.5, f32[24,128]{1,0:T(8,128)} %get-tuple-element.11.m_ref.own_ref, ...), custom_call_target="tpu_custom_call" | custom-call | flops 4000000000 | bytes 8000000 | tf_op jit(solution)/shard_map/pallas_call | solution.py:498
  76.5 0.0 collective-permute-done.refs_0_
  76.5 0.0 copy-start
  76.5 0.6 copy-done
  77.1 1.7 %shard_map.97 = bf16[128,1024]{1,0:T(8,128)(2,1)} custom-call(bf16[2,128,512]{2,1,0:T(8,128)(2,1)} %shard_map.96.chunk_ref, bf16[128,512]{1,0:T(8,128)(2,1)} %copy-done), custom_call_target="tpu_custom_call" | custom-call | tf_op jit(solution)/shard_map/pallas_call | solution.py:514
Async XLA Ops:
  62.2 14.3 %collective-permute-start = (bf16[128,512]{1,0:T(8,128)(2,1)S(1)}, bf16[128,512]{1,0:T(8,128)(2,1)S(1)}, u32[]{:S(2)}, u32[]{:S(2)}) collective-permute-start(bf16[128,512]{1,0:T(8,128)(2,1)S(1)} %slice_bitcast_fusion), channel_id=1, source_target_pairs={{0,1},{1,0},{2,3},{3,2},{4,5},{5,4},{6,7},{7,6},{8,9},{9,8},{10,11... | collective-permute-start | bytes 393224 | tf_op jit(solution)/shard_map/ppermute | solution.py:494
  76.5 0.7 copy-start

commit v5 on v3

--- a/solution.py
+++ b/solution.py
@@ -8,7 +8,7 @@
 from jax.sharding import PartitionSpec as P
 
 GROUP = 4
-JOBS_STEP = 4
+JOBS_STEP = 6
 PER_PEER = 2
 MESH_ID = pl.DeviceIdType.MESH
 NT = (((1,), (1,)), ((), ()))

time: 78.2 us -> 78.2 us (level)
  the two profiles are of different devices: /device:TPU:0 before, /device:TPU:9 now
where the time goes in v5:
time: 78.2 us; the launch traced here: 77.9 us
  Pallas kernels  74.3 us (95%)
  local copies, waits for them, and re-layouts  1.56 us (2%)
  starting transfers between devices  1.3 us (2%)
    pallas_call x1, Pallas kernels, gather(): pl.pallas_call(functools.partial(gather_kernel, count // GROUP), out_shap...  54.5 us
    pallas_call x1, Pallas kernels, shards(): pl.pallas_call(functools.partial(owner_kernel, blocks, heads, block_len,...  10.4 us
    pallas_call x1, Pallas kernels, shards(): pl.pallas_call(functools.partial(query_kernel, blocks, heads, top, block_...  5.72 us
    pallas_call x1, Pallas kernels, shards(): pl.pallas_call(functools.partial(prep_kernel, blocks, heads, top, block_l...  1.99 us
    pallas_call x1, Pallas kernels, shards(): pl.pallas_call(join_kernel, out_shape=jax.ShapeDtypeStruct((row_count //...  1.71 us
  transfers between devices with their start and end apart: 1, of which 0 were waited for; matrix products, arithmetic and copies ran while one was open for 0% of the time, Pallas kernels for 13%

profile of v5, /device:TPU:9, one launch (start us, length us, event | category | flops | bytes accessed | tf_op | source)
XLA Modules:
  0.0 77.9 jit_solution(3634686397749872711)
XLA Ops:
  0.6 2.0 %shard_map.94 = (f32[256,8]{1,0:T(8,128)}, f32[24,128]{1,0:T(8,128)}) custom-call(s32[3,2,4]{2,1,0:T(2,128)} %bitcast.4, bf16[256,512]{1,0:T(8,128)(2,1)} %g_ref.7, bf16[256,512]{1,0:T(8,128)(2,1)} %o_ref.1, f32[4,256]{1,0:T(4,128)} %bitcast.6), custom_call_target="tpu_custom_call" | custom-call | tf_op jit(solution)/shard_map/pallas_call | solution.py:467
  2.6 54.5 %shard_map.95 = (bf16[16,256,512]{2,1,0:T(8,128)(2,1)}, bf16[16,256,512]{2,1,0:T(8,128)(2,1)}, f32[16,24,128]{2,1,0:T(8,128)}) custom-call(bf16[256,512]{1,0:T(8,128)(2,1)} %q_ref.5, bf16[256,512]{1,0:T(8,128)(2,1)} %g_ref.7, bf16[256,512]{1,0:T(8,128)(2,1)} %k_ref.5, bf16[256,512]{1,0:T(8,128)(2,1)} %v_ref.5, f32[24,128]{1,0:T(8,128)} %get-tuple-element.11.m_ref.own_ref), custom_call_target="tpu_custom_call" | custom-call | tf_op jit(solution)/shard_map/pallas_call | solution.py:222
  57.1 5.7 %shard_map.96.chunk_ref = bf16[2,128,512]{2,1,0:T(8,128)(2,1)} custom-call(s32[3,2,4]{2,1,0:T(2,128)} %bitcast.5, bf16[256,512]{1,0:T(8,128)(2,1)} %q_ref.5, bf16[256,512]{1,0:T(8,128)(2,1)} %g_ref.7, bf16[256,512]{1,0:T(8,128)(2,1)} %k_ref.5, bf16[256,512]{1,0:T(8,128)(2,1)} %v_ref.5, f32[256,8]{1,0:T(8,128)} %get-tuple-element.10.stat_ref, ...), custom_call_target="tpu_custom_call" | custom-call | flops 1000000000 | bytes 4000000 | tf_op jit(solution)/shard_map/pallas_call | solution.py:481
  62.9 0.9 %slice_bitcast_fusion = bf16[128,512]{1,0:T(8,128)(2,1)S(1)} fusion(bf16[2,128,512]{2,1,0:T(8,128)(2,1)} %shard_map.96.chunk_ref), kind=kLoop, calls=%fused_computation | loop fusion | bytes 262144 | tf_op jit(solution)/shard_map/squeeze | solution.py:492
  63.8 1.3 %collective-permute-start = (bf16[128,512]{1,0:T(8,128)(2,1)S(1)}, bf16[128,512]{1,0:T(8,128)(2,1)S(1)}, u32[]{:S(2)}, u32[]{:S(2)}) collective-permute-start(bf16[128,512]{1,0:T(8,128)(2,1)S(1)} %slice_bitcast_fusion), channel_id=1, source_target_pairs={{0,1},{1,0},{2,3},{3,2},{4,5},{5,4},{6,7},{7,6},{8,9},{9,8},{10,11... | collective-permute-start | bytes 393224 | tf_op jit(solution)/shard_map/ppermute | solution.py:492
  65.1 10.4 %shard_map.98 = (bf16[256,512]{1,0:T(8,128)(2,1)}, bf16[256,512]{1,0:T(8,128)(2,1)}) custom-call(bf16[256,512]{1,0:T(8,128)(2,1)} %q_ref.5, bf16[256,512]{1,0:T(8,128)(2,1)} %g_ref.7, bf16[256,512]{1,0:T(8,128)(2,1)} %k_ref.5, bf16[256,512]{1,0:T(8,128)(2,1)} %v_ref.5, f32[24,128]{1,0:T(8,128)} %get-tuple-element.11.m_ref.own_ref, ...), custom_call_target="tpu_custom_call" | custom-call | flops 4000000000 | bytes 8000000 | tf_op jit(solution)/shard_map/pallas_call | solution.py:496
  75.5 0.0 collective-permute-done.refs_0_
  75.5 0.0 copy-start
  75.5 0.6 copy-done
  76.2 1.7 %shard_map.97 = bf16[128,1024]{1,0:T(8,128)(2,1)} custom-call(bf16[2,128,512]{2,1,0:T(8,128)(2,1)} %shard_map.96.chunk_ref, bf16[128,512]{1,0:T(8,128)(2,1)} %copy-done), custom_call_target="tpu_custom_call" | custom-call | tf_op jit(solution)/shard_map/pallas_call | solution.py:512
Async XLA Ops:
  63.8 11.7 %collective-permute-start = (bf16[128,512]{1,0:T(8,128)(2,1)S(1)}, bf16[128,512]{1,0:T(8,128)(2,1)S(1)}, u32[]{:S(2)}, u32[]{:S(2)}) collective-permute-start(bf16[128,512]{1,0:T(8,128)(2,1)S(1)} %slice_bitcast_fusion), channel_id=1, source_target_pairs={{0,1},{1,0},{2,3},{3,2},{4,5},{5,4},{6,7},{7,6},{8,9},{9,8},{10,11... | collective-permute-start | bytes 393224 | tf_op jit(solution)/shard_map/ppermute | solution.py:492
  75.5 0.7 copy-start
